TPU v7x, 32 devices: a whole 2x2x4 slice. The times are simulated.
32 devices in a mesh: sys: 2 (over x), aux: 4 (over z), orb: 4 (over y, core).
Axes of the slice: x: 2, y: 2, z: 4, core: 2. Of those that a mesh axis runs over, the one named last changes fastest.
Arguments:
- aux_ints: float32 [928, 232, 232], P(('sys', 'aux'), 'orb'), parts along dimension 0
- metric: float32 [928, 464], P(('sys', 'aux')), parts along dimension 0
- orbitals: float32 [16, 232, 20], P('sys'), parts along dimension 0
Outputs:
- output: float32 [16, 232, 232], P('sys', 'orb', 'aux'), parts along dimension 0
There are 2 independent parts. A program takes and returns all parts, laid end to end along the dimension named above; each array names one.
All inputs are finite; a program needn't handle non-finite values.
Results may differ from a plain program's by a relative error of at most 0.001.
Values are sent between devices in bfloat16 or wider.
A program may use at most 1 GiB of HBM per device.

v0:
```python
import jax
import jax.numpy as jnp
from jax import lax
from jax.sharding import PartitionSpec as P

PRECISE = lax.Precision.HIGHEST


def solution(mesh):
    def local_fock(ints_blk, metric_blk, orbitals):
        m_loc = ints_blk.shape[1]
        row_start = lax.axis_index('orb') * m_loc
        half_tr = jnp.einsum('qml,dli->qmdi', ints_blk, orbitals, precision=PRECISE, preferred_element_type=jnp.float32)
        orb_rows = lax.dynamic_slice_in_dim(orbitals, row_start, m_loc, axis=1)
        gamma_part = jnp.einsum('qmdi,dmi->dq', half_tr, orb_rows, precision=PRECISE, preferred_element_type=jnp.float32)
        gamma_raw = lax.psum(gamma_part, 'orb')
        gamma_all = lax.all_gather(gamma_raw, 'aux', axis=1, tiled=True)
        gamma_fit = jnp.einsum('dq,pq->dp', gamma_all, metric_blk, precision=PRECISE, preferred_element_type=jnp.float32)
        weight_part = jnp.dot(gamma_fit, metric_blk, precision=PRECISE, preferred_element_type=jnp.float32)
        weights = lax.psum_scatter(weight_part, 'aux', scatter_dimension=1, tiled=True)
        coulomb = jnp.einsum('dq,qmn->dmn', weights, ints_blk, precision=PRECISE, preferred_element_type=jnp.float32)
        half_all = lax.all_gather(half_tr, 'aux', axis=0, tiled=True)
        fitted = jnp.einsum('pq,qmdi->pmdi', metric_blk, half_all, precision=PRECISE, preferred_element_type=jnp.float32)
        fitted_all = lax.all_gather(fitted, 'orb', axis=1, tiled=True)
        exchange = jnp.einsum('pmdi,pndi->dmn', fitted, fitted_all, precision=PRECISE, preferred_element_type=jnp.float32)
        fock_part = 2.0 * coulomb - exchange
        return lax.psum_scatter(fock_part, 'aux', scatter_dimension=2, tiled=True)

    return jax.shard_map(local_fock, mesh=mesh, in_specs=(P(('sys', 'aux'), 'orb', None), P(('sys', 'aux'), None), P('sys', None, None)), out_specs=P('sys', 'orb', 'aux'), check_vma=False)
```

profile of v0, /device:TPU:0, one launch (start us, length us, event | category | flops | bytes accessed | tf_op | source)
XLA Modules:
  0.0 949.0 jit_solution(9688110850015234397)
XLA Ops:
  6.5 0.0 copy-start
  6.5 0.0 all-gather.4.cloned.1.call-start
  6.5 11.0 %fusion.2 = f32[116,58,8,20]{0,3,2,1:T(8,128)} fusion(f32[116,58,232]{0,2,1:T(8,128)} %param.3, f32[8,232,20]{1,0,2:T(8,128)} %param.5), kind=kOutput, calls=%fused_computation.2 | convolution fusion | flops 2996920320 | bytes 10697984 | tf_op jit(solution)/shard_map/qml,dli->qmdi/dot_general | solution.py:13
  17.6 11.7 %copy.16 = f32[116,58,8,20]{1,2,3,0:T(8,128)} copy(f32[116,58,8,20]{0,3,2,1:T(8,128)} %fusion.2) | data formatting | bytes 8611840 | tf_op jit(solution)/shard_map/qml,dli->qmdi/dot_general | solution.py:13
  29.2 0.0 all-gather.4.cloned.1.call-update
  29.3 0.2 all-gather.6.cloned.1.call-start
  29.5 639.3 %all-gather.4.cloned.1.call-done = f32[464,58,8,20]{1,2,3,0:T(8,128)} async-done(((f32[116,58,8,20]{1,2,3,0:T(8,128)}), f32[464,58,8,20]{1,2,3,0:T(8,128)}) %all-gather.4.cloned.1.call-update) | async-done | bytes 17223696 | tf_op jit(solution)/shard_map/all_gather | solution.py:22
  668.7 36.3 %copy.17 = f32[464,58,8,20]{0,3,2,1:T(8,128)} copy(f32[464,58,8,20]{1,2,3,0:T(8,128)} %all-gather.4.cloned.1.call-done) | data formatting | bytes 34447360 | tf_op jit(solution)/shard_map/all_gather | solution.py:22
  705.0 0.0 copy-done
  705.0 21.5 %convolution_bitcast_fusion = f32[116,58,8,20]{0,3,2,1:T(8,128)S(1)} fusion(f32[464,58,8,20]{0,3,2,1:T(8,128)} %copy.17, f32[116,464]{0,1:T(8,128)S(1)} %copy-done), kind=kOutput, calls=%fused_computation.7 | convolution fusion | flops 5993840640 | bytes 21744896 | tf_op jit(solution)/shard_map/pq,qmdi->pmdi/dot_general | solution.py:23
  726.5 0.0 copy-start.1
  726.6 2.4 copy-done.1
  728.9 0.0 copy-start.2
  729.0 3.1 copy.18
  732.1 0.0 copy-start.3
  732.1 0.0 all-gather.6.cloned.1.call-update
  732.1 0.0 all-reduce.4.cloned.1.call-start
  732.2 0.0 copy-done.2
  732.2 0.1 dynamic-slice_bitcast_fusion
  732.3 8.6 fusion.4
  740.9 6.3 psum.7
  747.3 13.0 %all-gather = f32[4,116,8]{1,2,0:T(8,128)S(1)} all-gather(f32[1,116,8]{1,2,0:T(8,128)S(1)} %bitcast.45), channel_id=1, replica_groups=mesh['sys'=2,'aux'=4,'orb'=4] {'aux'}, dimensions={0}, use_global_device_ids=true | all-gather | bytes 18560 | tf_op jit(solution)/shard_map/all_gather | solution.py:17
  760.3 0.1 reshape.1
  760.4 0.0 copy-done.3
  760.4 0.6 dynamic-slice
  761.6 0.2 fusion.18
  761.9 0.4 fusion.19
  762.3 16.9 %all-reduce = f32[8,464]{1,0:T(8,128)S(1)} all-reduce(f32[8,464]{1,0:T(8,128)S(1)} %fusion.19), channel_id=2, replica_groups=mesh['sys'=2,'aux'=4,'orb'=4] {'aux'}, use_global_device_ids=true, to_apply=%region_1.0.clone | all-reduce | flops 3712 | bytes 29696
  779.2 73.4 %all-gather.6.cloned.1.call-done = f32[116,232,8,20]{0,2,3,1:T(8,128)} async-done(((f32[116,58,8,20]{0,2,3,1:T(8,128)}), f32[116,232,8,20]{0,2,3,1:T(8,128)}) %all-gather.6.cloned.1.call-update) | async-done | bytes 17223696 | tf_op jit(solution)/shard_map/all_gather | solution.py:24
  852.5 35.0 %fusion.7 = f32[8,58,232]{2,1,0:T(8,128)S(1)} fusion(f32[116,232,8,20]{0,2,3,1:T(8,128)} %all-gather.6.cloned.1.call-done, f32[116,58,8,20]{0,3,2,1:T(8,128)} %copy-done.1), kind=kOutput, calls=%fused_computation.8 | convolution fusion | flops 2996920320 | bytes 21960192 | tf_op jit(solution)/shard_map/pmdi,pndi->dmn/dot_general | solution.py:25
  887.6 14.5 %fusion.12 = f32[8,58,232]{2,0,1:T(8,128)} fusion(f32[116,58,232]{0,2,1:T(8,128)} %param.3, f32[8,58,232]{2,1,0:T(8,128)S(1)} %fusion.7, f32[8,464]{1,0:T(8,128)S(1)} %all-reduce, u32[]{:T(128)S(6)} %multiply.1), kind=kOutput, calls=%fused_computation.10 | convolution fusion | flops 150061312 | bytes 7202564 | tf_op jit(solution)/shard_map/dq,qmn->dmn/dot_general | solution.py:21
  902.1 0.0 all-reduce.4.cloned.1.call-update
  902.8 37.4 %all-reduce.4.cloned.1.call-done = f32[8,58,232]{2,0,1:T(8,128)} async-done(((f32[8,58,232]{2,0,1:T(8,128)}), f32[8,58,232]{2,0,1:T(8,128)}) %all-reduce.4.cloned.1.call-update) | async-done | bytes 430608
  940.2 1.8 constant_dynamic-slice_fusion
  (1 shorter events, 0.0 us)
Async XLA Ops:
  6.5 698.5 %copy-start = (f32[116,464]{0,1:T(8,128)S(1)}, f32[116,464]{0,1:T(8,128)}, u32[]{:S(2)}) copy-start(f32[116,464]{0,1:T(8,128)} %param.4) | copy-start | bytes 645892
  6.5 662.2 %all-gather.4.cloned.1.call-start = ((), (), s32[]{:S(2)}) async-start(), calls=%async_computation | async-start | bytes 47513600 | tf_op jit(solution)/shard_map/all_gather | solution.py:22
  29.3 823.3 %all-gather.6.cloned.1.call-start = ((), (), s32[]{:S(2)}) async-start(), calls=%async_computation.1 | async-start | bytes 23756800 | tf_op jit(solution)/shard_map/all_gather | solution.py:24
  726.5 2.4 copy-start.1
  728.9 3.2 copy-start.2
  732.1 28.3 %copy-start.3 = (u32[32]{0:T(128)S(1)}, u32[32]{0:T(128)}, u32[]{:S(2)}) copy-start(u32[32]{0:T(128)} %constant.16) | copy-start | bytes 388
  732.1 208.0 %all-reduce.4.cloned.1.call-start = ((), (), s32[]{:S(2)}) async-start(), calls=%async_computation.2 | async-start | bytes 950272
Sparse Core Ops, SparseCore 0:
  29.4 639.3 all-gather.3
  732.2 120.2 all-gather.5
  902.3 37.8 all-reduce.3
where the time goes:
time: 955 us; the launch traced here: 949 us
  waiting for transfers between devices  750 us (79%)
  matrix products  91.4 us (10%)
  local copies, waits for them, and re-layouts  56.1 us (6%)
  blocking collectives  36.3 us (4%)
  between operations  14.9 us (2%)
    all_gather x1, waiting for transfers between devices, local_fock(): half_all = lax.all_gather(half_tr, 'aux', axis=0, tiled=True)  639 us
    all_gather x1, waiting for transfers between devices, local_fock(): fitted_all = lax.all_gather(fitted, 'orb', axis=1, tiled=True)  73.4 us
    unnamed x4, waiting for transfers between devices  37.4 us
    all_gather x1, local copies, waits for them, and re-layouts, local_fock(): half_all = lax.all_gather(half_tr, 'aux', axis=0, tiled=True)  36.3 us
    dot_general x1, matrix products, local_fock(): jnp.einsum('pmdi,pndi->dmn', fitted, fitted_all, precision=PRECISE, prefe...  35 us
    dot_general x1, matrix products, local_fock(): jnp.einsum('pq,qmdi->pmdi', metric_blk, half_all, precision=PRECISE, pref...  21.5 us
  transfers between devices with their start and end apart: 3, of which 3 were waited for; matrix products, arithmetic and copies ran while one was open for 1% of the time, Pallas kernels for 0%

commit v1 on v0

v1 whole, which is shorter than its diff:
```python
import jax
import jax.numpy as jnp
from jax import lax
from jax.sharding import PartitionSpec as P

PRECISE = lax.Precision.HIGHEST
F32 = jnp.float32


def solution(mesh):
    na, no = mesh.shape['aux'], mesh.shape['orb']
    ng = na * no

    def local_fock(ints_blk, metric_blk, orbitals):
        nq, m_loc, nb = ints_blk.shape
        nd, _, ni = orbitals.shape
        ncol = nd * ni // ng
        a, o = lax.axis_index('aux'), lax.axis_index('orb')
        me = a * no + o
        row_start = o * m_loc
        half_tr = jnp.einsum('dli,qml->dimq', orbitals, ints_blk, precision=PRECISE, preferred_element_type=F32)
        orb_rows = lax.dynamic_slice_in_dim(orbitals, row_start, m_loc, axis=1)
        blocks = half_tr.reshape(ng, ncol, m_loc, nq)
        got = lax.all_to_all(blocks.astype(jnp.bfloat16), ('aux', 'orb'), split_axis=0, concat_axis=0, tiled=True).astype(F32)
        own = lax.dynamic_slice_in_dim(blocks, me, 1, axis=0)
        got = lax.dynamic_update_slice_in_dim(got, own, me, axis=0)
        metric = lax.all_gather(metric_blk, 'aux', axis=0, tiled=True)
        gamma_part = jnp.einsum('dimq,dmi->dq', half_tr, orb_rows, precision=PRECISE, preferred_element_type=F32)
        gamma_raw = lax.psum(gamma_part, 'orb')
        gamma_all = lax.all_gather(gamma_raw, 'aux', axis=1, tiled=True)
        gamma_fit = jnp.einsum('dq,pq->dp', gamma_all, metric, precision=PRECISE, preferred_element_type=F32)
        weights = jnp.einsum('dp,qp->dq', gamma_fit, metric_blk, precision=PRECISE, preferred_element_type=F32)
        coulomb = jnp.einsum('dq,qmn->dmn', weights, ints_blk, precision=PRECISE, preferred_element_type=F32)
        cols = got.reshape(na, no, ncol, m_loc, nq).transpose(2, 1, 3, 0, 4).reshape(ncol, nb, na * nq)
        fitted = jnp.einsum('cmq,pq->cmp', cols, metric, precision=PRECISE, preferred_element_type=F32)
        kpart = jnp.einsum('cmp,cnp->mn', fitted, fitted, precision=PRECISE, preferred_element_type=F32)
        kp = kpart.reshape(no, m_loc, na, nb // na).transpose(2, 0, 1, 3).reshape(ng, m_loc, nb // na)
        kg = lax.all_to_all(kp, ('aux', 'orb'), split_axis=0, concat_axis=0, tiled=True)
        exchange = kg.reshape(nd, ng // nd, m_loc, nb // na).sum(1)
        return 2.0 * lax.psum_scatter(coulomb, 'aux', scatter_dimension=2, tiled=True) - exchange

    return jax.shard_map(local_fock, mesh=mesh, in_specs=(P(('sys', 'aux'), 'orb', None), P(('sys', 'aux'), None), P('sys', None, None)), out_specs=P('sys', 'orb', 'aux'), check_vma=False)
```

time: 955 us -> 241 us (0.25)
  waiting for transfers between devices: 750 us -> 35.7 us
  blocking collectives: 36.3 us -> 98.1 us
  matrix products: 91.4 us -> 44.3 us
  local copies, waits for them, and re-layouts: 56.1 us -> 30.2 us
  starting transfers between devices: 0.26 us -> 12.2 us
    all_gather x2 -> x0, waiting for transfers between devices: 713 us -> none  [the longest x1 639 us: local_fock(): half_all = lax.all_gather(half_tr, 'aux', axis=0, tiled=True)]
    all_gather x0 -> x1, blocking collectives: none -> 78.8 us  [local_fock(): metric = lax.all_gather(metric_blk, 'aux', axis=0, tiled=True)]
    dot_general x6, matrix products: 76.8 us -> 29.8 us  [the longest x1 9.73 us: local_fock(): jnp.einsum('cmq,pq->cmp', cols, metric, precision=PRECISE, preferred_elem...]
    all_gather x1, local copies, waits for them, and re-layouts: 36.3 us -> 2.6 us  [local_fock(): metric = lax.all_gather(metric_blk, 'aux', axis=0, tiled=True)]
    unnamed x1 -> x0, blocking collectives: 16.9 us -> none
    dot_general x2 -> x0, local copies, waits for them, and re-layouts: 14.8 us -> none  [the longest x1 11.7 us: local_fock(): jnp.einsum('qml,dli->qmdi', ints_blk, orbitals, precision=PRECISE, prefer...]
    reshape x0 -> x5, local copies, waits for them, and re-layouts: none -> 13.8 us  [the longest x2 13.2 us: local_fock(): got.reshape(na, no, ncol, m_loc, nq).transpose(2, 1, 3, 0, 4)]
    all_to_all x0 -> x2, starting transfers between devices: none -> 11.9 us  [the longest x1 7.58 us: local_fock(): lax.all_to_all(blocks.astype(jnp.bfloat16), ('aux', 'orb'), split_axis=0,...]
  transfers between devices with their start and end apart: 3 -> 3, of which waited for: 3 -> 1; matrix products, arithmetic and copies ran while one was open for 1% -> 13% of each run, Pallas kernels for 0% -> 0%
where the time goes in v1:
time: 241 us
  blocking collectives  98.1 us (41%)
  matrix products  44.3 us (18%)
  waiting for transfers between devices  35.7 us (15%)
  local copies, waits for them, and re-layouts  30.2 us (13%)
  between operations  14.2 us (6%)
  starting transfers between devices  12.2 us (5%)
  other arithmetic  5.98 us (2%)
    all_gather x1, blocking collectives, local_fock(): metric = lax.all_gather(metric_blk, 'aux', axis=0, tiled=True)  78.8 us
    unnamed x2, waiting for transfers between devices  35.7 us
    dot_general x1, matrix products, local_fock(): jnp.einsum('dq,qmn->dmn', weights, ints_blk, precision=PRECISE, preferred...  14.5 us
    all_gather x1, blocking collectives, local_fock(): gamma_all = lax.all_gather(gamma_raw, 'aux', axis=1, tiled=True)  13.5 us
    reshape x2, local copies, waits for them, and re-layouts, local_fock(): got.reshape(na, no, ncol, m_loc, nq).transpose(2, 1, 3, 0, 4)  13.2 us
    dot_general x1, matrix products, local_fock(): jnp.einsum('cmq,pq->cmp', cols, metric, precision=PRECISE, preferred_elem...  9.73 us
    unnamed x16, local copies, waits for them, and re-layouts  9.45 us
    dot_general x1, matrix products, local_fock(): jnp.einsum('dli,qml->dimq', orbitals, ints_blk, precision=PRECISE, prefer...  8.25 us
  transfers between devices with their start and end apart: 3, of which 1 were waited for; matrix products, arithmetic and copies ran while one was open for 13% of the time, Pallas kernels for 0%

profile of v1, /device:TPU:0, one launch (start us, length us, event | category | flops | bytes accessed | tf_op | source)
XLA Modules:
  0.0 240.7 jit_solution(1022089648848624883)
XLA Ops:
  6.5 8.3 %fusion.2 = f32[8,20,58,116]{3,1,0,2:T(8,128)S(1)} fusion(f32[116,58,232]{0,2,1:T(8,128)} %param.3, f32[8,232,20]{1,0,2:T(8,128)} %param.5), kind=kOutput, calls=%fused_computation.3 | convolution fusion | flops 2996920320 | bytes 10697984 | tf_op jit(solution)/shard_map/dli,qml->dimq/dot_general | solution.py:21
  14.8 2.8 %copy.29 = f32[8,20,58,116]{3,2,1,0:T(8,128)S(1)} copy(f32[8,20,58,116]{3,1,0,2:T(8,128)S(1)} %fusion.2) | data formatting | bytes 8611840 | tf_op jit(solution)/shard_map/dli,qml->dimq/transpose | solution.py:21
  17.6 0.0 copy-start
  17.6 2.3 copy-done
  19.9 0.0 copy-start.2
  19.9 2.2 convert_element_type.6
  22.1 0.0 copy-start.3
  22.1 7.6 %all-to-all-start = ((bf16[16,10,58,116]{3,2,1,0:T(8,128)(2,1)}), bf16[16,10,58,116]{3,2,1,0:T(8,128)(2,1)S(1)}, u32[]{:S(2)}, u32[]{:S(2)}) async-start(bf16[16,10,58,116]{3,2,1,0:T(8,128)(2,1)} %convert_element_type.6), calls=%async_computation | async-start | bytes 5242880 | tf_op jit(solution)/shard_map/all_to_all | solution.py:24
  29.7 0.0 copy-done.2
  29.7 78.8 %all-gather.1 = f32[4,116,464]{1,2,0:T(8,128)} all-gather(f32[1,116,464]{1,2,0:T(8,128)S(1)} %bitcast.58), channel_id=1, replica_groups=mesh['sys'=2,'aux'=4,'orb'=4] {'aux'}, dimensions={0}, use_global_device_ids=true | all-gather | bytes 1076480 | tf_op jit(solution)/shard_map/all_gather | solution.py:27
  108.5 2.6 %copy.28 = f32[4,116,464]{2,1,0:T(8,128)} copy(f32[4,116,464]{1,2,0:T(8,128)} %all-gather.1) | data formatting | bytes 1722368 | tf_op jit(solution)/shard_map/all_gather | solution.py:27
  111.1 2.3 reshape.33
  113.3 2.2 reshape.27
  115.6 0.0 copy-done.3
  115.6 0.1 dynamic-slice_bitcast_fusion
  115.7 5.4 %fusion.8 = f32[8,1,116,1]{2,1,3,0:T(1,128)S(1)} fusion(f32[8,20,58,116]{3,2,1,0:T(8,128)} %copy-done, f32[8,58,20,1]{1,0,2,3:T(8,128)S(1)} %dynamic-slice_bitcast_fusion), kind=kOutput, calls=%fused_computation.12 | convolution fusion | flops 12917760 | bytes 4346752 | tf_op jit(solution)/shard_map/dimq,dmi->dq/dot_general | solution.py:28
  121.1 5.8 %psum.7 = f32[8,116]{1,0:T(8,128)S(1)} all-reduce(f32[8,116]{1,0:T(8,128)S(1)} %bitcast.59), channel_id=1, replica_groups=mesh['sys'=2,'aux'=4,'orb'=4] {'orb'}, use_global_device_ids=true, to_apply=%region_0.0 | all-reduce | flops 928 | bytes 7424 | tf_op jit(solution)/shard_map/psum | solution.py:29
  126.8 13.5 %all-gather = f32[4,116,8]{1,2,0:T(8,128)S(1)} all-gather(f32[1,116,8]{1,2,0:T(8,128)S(1)} %bitcast.60), channel_id=1, replica_groups=mesh['sys'=2,'aux'=4,'orb'=4] {'aux'}, dimensions={0}, use_global_device_ids=true | all-gather | bytes 18560 | tf_op jit(solution)/shard_map/all_gather | solution.py:30
  140.4 0.1 reshape.25
  140.4 2.0 fusion.10
  142.5 0.3 convolution_bitcast_fusion.1
  142.8 0.0 all-to-all-done
  142.8 0.7 convert_element_type.7
  143.4 1.0 dynamic-slice_dynamic-update-slice_fusion
  144.4 6.4 %copy.47 = f32[4,4,10,58,116]{4,0,3,1,2:T(4,128)} copy(f32[4,4,10,58,116]{4,3,2,1,0:T(8,128)S(1)} %bitcast.55) | data formatting | bytes 8611840 | tf_op jit(solution)/shard_map/reshape | solution.py:34
  150.9 0.0 copy-start.1
  150.9 6.8 %reshape.20 = f32[10,232,464]{2,1,0:T(8,128)} reshape(f32[10,4,58,4,116]{4,3,2,1,0:T(4,128)} %bitcast.56) | data formatting | bytes 8611840 | tf_op jit(solution)/shard_map/reshape | solution.py:34
  157.7 0.0 copy-done.1
  157.7 9.7 %fusion.12 = f32[10,232,464]{2,1,0:T(8,128)S(1)} fusion(f32[10,232,464]{2,1,0:T(8,128)} %reshape.20, f32[464,464,1]{1,0,2:T(8,128)S(1)} %copy-done.1), kind=kOutput, calls=%fused_computation.17 | convolution fusion | flops 5993840640 | bytes 9473024 | tf_op jit(solution)/shard_map/cmq,pq->cmp/dot_general | solution.py:35
  167.4 4.1 %convolution_bitcast_fusion = f32[232,232]{1,0:T(8,128)S(1)} fusion(f32[10,232,464]{2,1,0:T(8,128)S(1)} %fusion.12), kind=kOutput, calls=%fused_computation.4 | convolution fusion | flops 2996920320 | bytes 4521216 | tf_op jit(solution)/shard_map/cmp,cnp->mn/dot_general | solution.py:36
  171.5 0.3 reshape.21
  171.8 0.1 copy.31
  171.9 0.0 copy-start.4
  171.9 0.2 copy.32
  172.1 1.3 reshape.39
  173.4 4.3 %all-to-all-start.1 = ((f32[16,1,3364]{2,1,0:T(1,128)}), f32[16,1,3364]{2,1,0:T(1,128)S(1)}, u32[]{:S(2)}, u32[]{:S(2)}) async-start(f32[16,1,3364]{2,1,0:T(1,128)} %reshape.39), calls=%async_computation.1 | async-start | bytes 442368 | tf_op jit(solution)/shard_map/all_to_all | solution.py:38
  177.7 0.3 all-reduce.3.cloned.1.call-start
  178.0 14.5 %fusion.11 = f32[8,58,232]{2,0,1:T(8,128)} fusion(f32[8,116,1]{1,0,2:T(8,128)S(1)} %convolution_bitcast_fusion.1, f32[116,58,232]{0,2,1:T(8,128)} %param.3), kind=kOutput, calls=%fused_computation.16 | convolution fusion | flops 149846016 | bytes 6677888 | tf_op jit(solution)/shard_map/dq,qmn->dmn/dot_general | solution.py:33
  192.5 0.0 all-reduce.3.cloned.1.call-update
  192.6 0.0 copy-done.4
  192.6 0.6 dynamic-slice
  193.8 0.0 all-to-all-done.1
  193.8 0.5 broadcast
  194.4 1.2 reduce
  195.5 0.6 reshape.40
  196.2 35.7 %all-reduce.3.cloned.1.call-done = f32[8,58,232]{2,0,1:T(8,128)} async-done(((f32[8,58,232]{2,0,1:T(8,128)}), f32[8,58,232]{2,0,1:T(8,128)}) %all-reduce.3.cloned.1.call-update) | async-done | bytes 430608
  231.9 1.9 fusion.5
  (2 shorter events, 0.0 us)
Async XLA Ops:
  17.6 2.3 copy-start
  19.9 9.8 %copy-start.2 = (f32[116,464]{0,1:T(8,128)S(1)}, f32[116,464]{0,1:T(8,128)}, u32[]{:S(2)}) copy-start(f32[116,464]{0,1:T(8,128)} %param.4) | copy-start | bytes 645892
  22.1 93.5 %copy-start.3 = (f32[8,232,20]{1,0,2:T(8,128)S(1)}, f32[8,232,20]{1,0,2:T(8,128)}, u32[]{:S(2)}) copy-start(f32[8,232,20]{1,0,2:T(8,128)} %param.5) | copy-start | bytes 445444
  22.1 120.7 %all-to-all-start = ((bf16[16,10,58,116]{3,2,1,0:T(8,128)(2,1)}), bf16[16,10,58,116]{3,2,1,0:T(8,128)(2,1)S(1)}, u32[]{:S(2)}, u32[]{:S(2)}) async-start(bf16[16,10,58,116]{3,2,1,0:T(8,128)(2,1)} %convert_element_type.6), calls=%async_computation | async-start | bytes 5242880 | tf_op jit(solution)/shard_map/all_to_all | solution.py:24
  150.9 6.8 %copy-start.1 = (f32[464,464,1]{1,0,2:T(8,128)S(1)}, f32[464,464,1]{1,0,2:T(8,128)}, u32[]{:S(2)}) copy-start(f32[464,464,1]{1,0,2:T(8,128)} %reshape.33) | copy-start | bytes 2583556
  171.9 20.6 %copy-start.4 = (u32[32]{0:T(128)S(1)}, u32[32]{0:T(128)}, u32[]{:S(2)}) copy-start(u32[32]{0:T(128)} %constant.25) | copy-start | bytes 388
  173.4 20.4 %all-to-all-start.1 = ((f32[16,1,3364]{2,1,0:T(1,128)}), f32[16,1,3364]{2,1,0:T(1,128)S(1)}, u32[]{:S(2)}, u32[]{:S(2)}) async-start(f32[16,1,3364]{2,1,0:T(1,128)} %reshape.39), calls=%async_computation.1 | async-start | bytes 442368 | tf_op jit(solution)/shard_map/all_to_all | solution.py:38
  177.7 54.2 %all-reduce.3.cloned.1.call-start = ((), (), s32[]{:S(2)}) async-start(), calls=%async_computation.2 | async-start | bytes 950272
Sparse Core Ops, SparseCore 0:
  192.7 39.2 all-reduce.2

commit v2 on v0

v2 whole, which is shorter than its diff:
```python
import jax
import jax.numpy as jnp
from jax import lax
from jax.experimental import pallas as pl
from jax.experimental.pallas import tpu as pltpu
from jax.sharding import PartitionSpec as P

F32 = jnp.float32
BF = jnp.bfloat16
MESH = pl.DeviceIdType.MESH
NN = (((1,), (0,)), ((), ()))
NT = (((1,), (1,)), ((), ()))
LANES = 128
MROW = 64
NT8 = 8
SP = 168


def split3(x):
    hi = x.astype(BF)
    rest = x - hi.astype(F32)
    mid = rest.astype(BF)
    return hi, mid, (rest - mid.astype(F32)).astype(BF)


def dot(x, y, dims):
    return lax.dot_general(x, y, dims, preferred_element_type=F32)


def lhs6(x, axis):
    h, m, l = x
    return jnp.concatenate([h, h, m, m, h, l], axis=axis)


def rhs6(x, axis):
    h, m, l = x
    return jnp.concatenate([h, m, h, m, l, h], axis=axis)


def kernel(nm, nl, nq, nd, ni, bt, mt, ct, out, bv, mv, cv, ctp, tr, sbuf, rbuf, own, mloc, mq, msp, gsend, grecv, jsend, jrecv, zbuf, kacc, kin, kful, kmsg, krecv, gbuf,
           bsem, lsem, tsend, trecv, mzsend, mzrecv, mosend, morecv, gssem, grsem, jssem, jrsem, kxs, kxr, kss, krs):
    sy, a, o = lax.axis_index('sys'), lax.axis_index('aux'), lax.axis_index('orb')
    me = a * 4 + o
    dens, half = me // 2, me % 2
    nh = ni // 2
    npair = nh // 2

    def dev(aa, oo):
        return (sy, aa, oo)

    pltpu.make_async_copy(ct, cv, lsem.at[0]).start()
    for t in range(NT8):
        n = min(8, nm - 8 * t)
        pltpu.make_async_copy(bt.at[pl.ds(8 * t, n)], bv.at[pl.ds(8 * t, n)], bsem.at[t]).start()
        if t == 0:
            pltpu.make_async_copy(mt, mv, lsem.at[1]).start()
    barrier = pltpu.get_barrier_semaphore()

    def tell(k, c):
        g = lax.rem(me + k, 16)
        pl.semaphore_signal(barrier, inc=1, device_id=dev(g // 4, g % 4), device_id_type=MESH)
        return c
    lax.fori_loop(1, 16, tell, 0)

    pltpu.make_async_copy(ct, cv, lsem.at[0]).wait()
    ctp[...] = jnp.concatenate([cv[...], jnp.zeros((nd * ni, 256 - nl), F32)], axis=1)
    lhs = lhs6(split3(ctp[...]), 1)
    pltpu.make_async_copy(mt, mv, lsem.at[1]).wait()
    for b in range(4):
        blk = jnp.concatenate([mv[nq * b:nq * (b + 1), :], jnp.zeros((nq, LANES - nq), F32)], axis=1)
        mloc[b] = jnp.concatenate([blk, jnp.zeros((LANES - nq, LANES), F32)], axis=0)
    pl.semaphore_wait(barrier, 15)

    def mz(j, c):
        aa = lax.rem(a + j, 4)
        pltpu.make_async_remote_copy(src_ref=mloc.at[o], dst_ref=mq.at[a, o], send_sem=mzsend, recv_sem=mzrecv,
                                     device_id=dev(aa, o), device_id_type=MESH).start()
        return c
    lax.fori_loop(1, 4, mz, 0)

    gam = jnp.zeros((nd, LANES), F32)
    tr2 = tr

    def tile(t, pairs, gam):
        n = 2 * pairs
        pltpu.make_async_copy(bt.at[pl.ds(0, n)], bv.at[pl.ds(0, n)], bsem.at[t]).wait()
        cols = pltpu.roll(ctp[...], lax.rem(512 - (nm * o + 8 * t), 256), 1)
        for r in range(0, n, 2):
            x = jnp.concatenate([jnp.concatenate([bv[8 * t + r + e], jnp.zeros((nl, LANES - nq), F32)], axis=1) for e in range(2)], axis=1)
            x = jnp.concatenate([x, jnp.zeros((256 - nl, 2 * LANES), F32)], axis=0)
            y = dot(lhs, rhs6(split3(x), 0), NN)
            for e in range(2):
                ye = y[:, e * LANES:(e + 1) * LANES]
                tr2[pl.ds((r + e) * SP, nd * ni), :] = ye
                w = ye * cols[:, r + e:r + e + 1]
                gam = gam + w.reshape(ni, nd, LANES).sum(0)
        for g in range(16):
            d, h = g // 2, g % 2
            for p in range(npair):
                two = [tr2[pl.ds((h * nh + 2 * p + e) * nd + d, 8, stride=SP), :] for e in range(2)]
                sbuf[g, p, t] = jnp.concatenate(two, axis=0).astype(BF)
        for p in range(npair):
            two = [tr2[pl.ds((half * nh + 2 * p + e) * nd + dens, 8, stride=SP), :] for e in range(2)]
            _, mid, low = split3(jnp.concatenate(two, axis=0))
            own[0, p, t] = mid
            own[1, p, t] = low
        return gam

    def send_t1(p, t0, nt):
        def one(k, c):
            j, u = k // 4, k % 4
            aa = lax.rem(a + 2 + j, 4)
            oo = lax.rem(o + 1 + u, 4)
            g = aa * 4 + oo
            src = sbuf.at[g, p, pl.ds(t0, nt)]
            dst = rbuf.at[a, p, o, pl.ds(t0, nt)]

            @pl.when(k != 11)
            def _():
                pltpu.make_async_remote_copy(src_ref=src, dst_ref=dst, send_sem=tsend, recv_sem=trecv.at[p],
                                             device_id=dev(aa, oo), device_id_type=MESH).start()

            @pl.when(k == 11)
            def _():
                pltpu.make_async_copy(src, dst, trecv.at[p]).start()
            return c
        lax.fori_loop(0, 16, one, 0)

    def two_tiles(u, gam):
        gam = tile(2 * u, 4, gam)
        gam = tile(2 * u + 1, 4, gam)
        send_t1(0, 2 * u, 2)
        return gam
    gam = lax.fori_loop(0, 3, two_tiles, gam)
    gam = tile(6, 4, gam)
    gam = tile(7, 1, gam)
    send_t1(0, 6, 2)

    gsend[...] = gam

    def gs(k, c):
        g = lax.rem(me + k, 16)
        pltpu.make_async_remote_copy(src_ref=gsend, dst_ref=grecv.at[a, o], send_sem=gssem, recv_sem=grsem,
                                     device_id=dev(g // 4, g % 4), device_id_type=MESH).start()
        return c
    lax.fori_loop(1, 16, gs, 0)
    pltpu.make_async_copy(gsend, grecv.at[a, o], grsem).start()

    pltpu.make_async_copy(mq.at[pl.ds(0, 3), 0], mq.at[pl.ds(0, 3), 0], mzrecv).wait()

    def mo(k, c):
        aa, oo = lax.rem(a + 1 + k // 3, 4), lax.rem(o + 1 + k % 3, 4)
        pltpu.make_async_remote_copy(src_ref=mq.at[aa, o], dst_ref=mq.at[aa, o], send_sem=mosend, recv_sem=morecv,
                                     device_id=dev(a, oo), device_id_type=MESH).start()
        return c
    lax.fori_loop(0, 9, mo, 0)
    for p in range(1, npair):
        send_t1(p, 0, NT8)
    mq[a] = mloc[...]
    pltpu.make_async_copy(mq.at[pl.ds(0, 3), pl.ds(0, 3)], mq.at[pl.ds(0, 3), pl.ds(0, 3)], morecv).wait()
    for b in range(4):
        parts = split3(jnp.concatenate([mq[aa, b] for aa in range(4)], axis=1))
        for s in range(3):
            msp[s, pl.ds(b * LANES, LANES)] = parts[s]

    pltpu.make_async_copy(grecv, grecv, grsem).wait()
    graw = jnp.concatenate([grecv[aa, 0] + grecv[aa, 1] + grecv[aa, 2] + grecv[aa, 3] for aa in range(4)], axis=1)
    m3 = [msp[s] for s in range(3)]
    gfit = dot(lhs6(split3(graw), 1), rhs6(m3, 0), NN)
    mown = split3(jnp.concatenate([mloc[b] for b in range(4)], axis=0))
    wts = dot(lhs6(split3(gfit), 1), rhs6(mown, 0), NN)
    wl = lhs6(split3(wts), 1)
    low64 = lax.broadcasted_iota(jnp.int32, (nd, LANES), 1) < 64

    def jpair(u, c):
        ys = []
        for e in range(2):
            x = jnp.concatenate([bv[2 * u + e], jnp.zeros((nl, LANES - nq), F32)], axis=1)
            x = jnp.concatenate([x, jnp.zeros((256 - nl, LANES), F32)], axis=0)
            ys.append(dot(wl, rhs6(split3(x), 1), NT))
        for aa in range(4):
            lo = pltpu.roll(ys[0], (256 - nm * aa) % 256, 1)[:, :LANES]
            hi = pltpu.roll(ys[1], (256 + 64 - nm * aa) % 256, 1)[:, :LANES]
            jsend[aa, u] = jnp.where(low64, lo, hi)
        return c

    def fit(p):
        pltpu.make_async_copy(rbuf.at[:, p], rbuf.at[:, p], trecv.at[p]).wait()
        for q in range(4):
            x = jnp.concatenate([rbuf[s, p, q].reshape(LANES, LANES) for s in range(4)], axis=1)
            z = dot(jnp.concatenate([x, x, x], axis=1), msp[...].reshape(3 * 512, 512), NN)
            zbuf[pl.ds(8 * q, 8)] = z.reshape(8, 2, 8, 512)
        mid, low = own[0, p].reshape(LANES, LANES), own[1, p].reshape(LANES, LANES)
        rows = pl.ds(pl.multiple_of(a * LANES, LANES), LANES)
        mh, mm = msp[0, rows], msp[1, rows]
        z = dot(jnp.concatenate([mid, mid, low], axis=1), jnp.concatenate([mh, mm, mh], axis=0), NN)
        mine = pl.ds(8 * o, 8)
        zbuf[mine] = zbuf[mine] + z.reshape(8, 2, 8, 512)
        for e in range(2):
            s3 = split3(zbuf[:, e].reshape(4 * MROW, 512))
            k = dot(lhs6(s3, 1), rhs6(s3, 1), NT)
            if p == 0 and e == 0:
                kacc[0] = k[:, :LANES]
                kacc[1] = k[:, LANES:]
            else:
                kacc[0] = kacc[0] + k[:, :LANES]
                kacc[1] = kacc[1] + k[:, LANES:]

    fit(0)
    lax.fori_loop(0, nm // 2, jpair, 0)

    def js(j, c):
        aa = lax.rem(a + j, 4)
        pltpu.make_async_remote_copy(src_ref=jsend.at[aa], dst_ref=jrecv.at[a], send_sem=jssem, recv_sem=jrsem,
                                     device_id=dev(aa, o), device_id_type=MESH).start()
        return c
    lax.fori_loop(1, 4, js, 0)
    pltpu.make_async_copy(jsend.at[a], jrecv.at[a], jrsem).start()
    for p in range(1, npair):
        fit(p)

    mate = o + 1 - 2 * half
    swap = pltpu.make_async_remote_copy(src_ref=kacc.at[1 - half], dst_ref=kin, send_sem=kxs, recv_sem=kxr,
                                        device_id=dev(a, mate), device_id_type=MESH)
    swap.start()
    swap.wait_recv()
    kful[...] = kacc[half] + kin[...]
    low32 = lax.broadcasted_iota(jnp.int32, (32, LANES), 1) < 64
    for oo in range(4):
        ev = kful[pl.ds(MROW * oo, 32, stride=2), :]
        od = kful[pl.ds(MROW * oo + 1, 32, stride=2), :]
        kmsg[0, oo] = jnp.where(low32, ev, pltpu.roll(od, 64, 1))
        kmsg[1, oo] = jnp.where(low32, pltpu.roll(ev, 64, 1), od)

    def ks(k, c):
        al, oo = k // 4, k % 4
        aa = 2 * half + al
        same = jnp.logical_and(aa == a, oo == o)

        @pl.when(jnp.logical_not(same))
        def _():
            pltpu.make_async_remote_copy(src_ref=kmsg.at[al, oo], dst_ref=krecv.at[pl.ds(dens * 32, 32)], send_sem=kss, recv_sem=krs,
                                         device_id=dev(aa, oo), device_id_type=MESH).start()

        @pl.when(same)
        def _():
            cp = pltpu.make_async_copy(kmsg.at[al, oo], krecv.at[pl.ds(dens * 32, 32)], krs)
            cp.start()
        return c
    lax.fori_loop(0, 8, ks, 0)

    pltpu.make_async_copy(jrecv, jrecv, jrsem).wait()
    pltpu.make_async_copy(krecv, krecv, krs).wait()
    for u in range(nm // 2):
        j = jrecv[0, u] + jrecv[1, u] + jrecv[2, u] + jrecv[3, u]
        g = 2.0 * j - krecv[pl.ds(u, nd, stride=32), :]
        out[2 * u] = g[:, :nm]
        out[2 * u + 1] = pltpu.roll(g, 64, 1)[:, :nm]

    pltpu.make_async_copy(sbuf.at[pl.ds(0, 15)], sbuf.at[pl.ds(0, 15)], tsend).wait()
    pltpu.make_async_copy(mq.at[pl.ds(0, 3), 0], mq.at[pl.ds(0, 3), 0], mzsend).wait()
    pltpu.make_async_copy(mq.at[pl.ds(0, 3), pl.ds(0, 3)], mq.at[pl.ds(0, 3), pl.ds(0, 3)], mosend).wait()
    pltpu.make_async_copy(gbuf, gbuf, gssem).wait()
    pltpu.make_async_copy(jsend.at[pl.ds(0, 3)], jsend.at[pl.ds(0, 3)], jssem).wait()
    swap.wait_send()
    inset = (a // 2) == half

    @pl.when(inset)
    def _():
        pltpu.make_async_copy(krecv.at[pl.ds(0, 224)], krecv.at[pl.ds(0, 224)], kss).wait()

    @pl.when(jnp.logical_not(inset))
    def _():
        pltpu.make_async_copy(krecv, krecv, kss).wait()


def solution(mesh):
    def local_fock(ints_blk, metric_blk, orbitals):
        nq, nm, nl = ints_blk.shape
        nd, _, ni = orbitals.shape
        bt = jnp.transpose(ints_blk, (1, 2, 0))
        mt = metric_blk.T
        ct = jnp.transpose(orbitals, (2, 0, 1)).reshape(ni * nd, nl)
        npair = ni // 4
        V = pltpu.VMEM
        dma = pltpu.SemaphoreType.DMA
        g = pl.pallas_call(
            lambda *refs: kernel(nm, nl, nq, nd, ni, *refs),
            out_shape=jax.ShapeDtypeStruct((nm, nd, nm), F32),
            in_specs=[pl.BlockSpec(memory_space=pl.ANY)] * 3,
            out_specs=pl.BlockSpec(memory_space=pltpu.VMEM),
            scratch_shapes=[
                V((nm, nl, nq), F32), V((4 * nq, nq), F32), V((ni * nd, nl), F32), V((ni * nd, 256), F32),
                V((8 * SP, LANES), F32), V((16, npair, NT8, 16, LANES), BF), V((4, npair, 4, NT8, 16, LANES), BF),
                V((2, npair, NT8, 16, LANES), BF), V((4, LANES, LANES), F32), V((4, 4, LANES, LANES), F32), V((3, 512, 512), BF),
                V((nd, LANES), F32), V((4, 4, nd, LANES), F32), V((4, nm // 2, nd, LANES), F32), V((4, nm // 2, nd, LANES), F32),
                V((32, 2, 8, 512), F32), V((2, 256, LANES), F32), V((256, LANES), F32), V((256, LANES), F32), V((2, 4, 32, LANES), F32),
                V((8 * 32, LANES), F32), V((15, nd, LANES), F32),
                dma((NT8,)), dma((2,)), dma, dma((npair,)), dma, dma, dma, dma, dma, dma, dma, dma, dma, dma, dma, dma],
            compiler_params=pltpu.CompilerParams(collective_id=0, has_side_effects=True, vmem_limit_bytes=60 * 2**20),
        )(bt, mt, ct)
        return jnp.transpose(g, (1, 0, 2))

    return jax.shard_map(local_fock, mesh=mesh, in_specs=(P(('sys', 'aux'), 'orb', None), P(('sys', 'aux'), None), P('sys', None, None)), out_specs=P('sys', 'orb', 'aux'), check_vma=False)
```

time: 955 us -> 88.2 us (0.09)
  waiting for transfers between devices: 750 us -> 0 us
  matrix products: 91.4 us -> 0 us
  Pallas kernels: 0 us -> 86.4 us
  local copies, waits for them, and re-layouts: 56.1 us -> 1.65 us
  blocking collectives: 36.3 us -> 0 us
  between operations: 14.9 us -> 0.01 us
    all_gather x2 -> x0, waiting for transfers between devices: 713 us -> none  [the longest x1 639 us: local_fock(): half_all = lax.all_gather(half_tr, 'aux', axis=0, tiled=True)]
    dot_general x7 -> x0, matrix products: 91.4 us -> none  [the longest x1 35 us: local_fock(): jnp.einsum('pmdi,pndi->dmn', fitted, fitted_all, precision=PRECISE, prefe...]
    pallas_call x0 -> x1, Pallas kernels: none -> 86.4 us  [local_fock(): pl.pallas_call(lambda *refs: kernel(nm, nl, nq, nd, ni, *refs), out_shape...]
    unnamed x4 -> x0, waiting for transfers between devices: 37.4 us -> none
    all_gather x2 -> x0, local copies, waits for them, and re-layouts: 36.3 us -> none  [the longest x1 36.3 us: local_fock(): half_all = lax.all_gather(half_tr, 'aux', axis=0, tiled=True)]
    unnamed x1 -> x0, blocking collectives: 16.9 us -> none
    dot_general x2 -> x0, local copies, waits for them, and re-layouts: 14.8 us -> none  [the longest x1 11.7 us: local_fock(): jnp.einsum('qml,dli->qmdi', ints_blk, orbitals, precision=PRECISE, prefer...]
    all_gather x1 -> x0, blocking collectives: 13 us -> none  [local_fock(): gamma_all = lax.all_gather(gamma_raw, 'aux', axis=1, tiled=True)]
  transfers between devices with their start and end apart: 3 -> 0, of which waited for: 3 -> 0; matrix products, arithmetic and copies ran while one was open for 1% -> 0% of each run, Pallas kernels for 0% -> 0%
where the time goes in v2:
time: 88.2 us; the launch traced here: 88.1 us
  Pallas kernels  86.4 us (98%)
  local copies, waits for them, and re-layouts  1.65 us (2%)
    pallas_call x1, Pallas kernels, local_fock(): pl.pallas_call(lambda *refs: kernel(nm, nl, nq, nd, ni, *refs), out_shape...  86.4 us

profile of v2, /device:TPU:0, one launch (start us, length us, event | category | flops | bytes accessed | tf_op | source)
XLA Modules:
  0.0 88.1 jit_solution(17645221723298574447)
XLA Ops:
  0.0 86.4 %shard_map.37 = f32[58,8,58]{2,1,0:T(8,128)} custom-call(f32[58,232,116]{2,1,0:T(8,128)} %bitcast.6, f32[464,116]{1,0:T(8,128)} %bitcast.8, f32[160,232]{1,0:T(8,128)} %bitcast.9), custom_call_target="tpu_custom_call" | custom-call | tf_op jit(solution)/shard_map/pallas_call | solution.py:287
  86.4 1.6 %copy.5 = f32[8,58,58]{2,0,1:T(8,128)} copy(f32[8,58,58]{2,0,1:T(8,128)} %bitcast.7) | data formatting | bytes 215296

commit v3 on v2

--- a/solution.py
+++ b/solution.py
@@ -108,19 +108,19 @@
 
     def send_t1(p, t0, nt):
         def one(k, c):
-            j, u = k // 4, k % 4
+            j, u = k % 4, k // 4
             aa = lax.rem(a + 2 + j, 4)
             oo = lax.rem(o + 1 + u, 4)
             g = aa * 4 + oo
             src = sbuf.at[g, p, pl.ds(t0, nt)]
             dst = rbuf.at[a, p, o, pl.ds(t0, nt)]
 
-            @pl.when(k != 11)
+            @pl.when(k != 14)
             def _():
                 pltpu.make_async_remote_copy(src_ref=src, dst_ref=dst, send_sem=tsend, recv_sem=trecv.at[p],
                                              device_id=dev(aa, oo), device_id_type=MESH).start()
 
-            @pl.when(k == 11)
+            @pl.when(k == 14)
             def _():
                 pltpu.make_async_copy(src, dst, trecv.at[p]).start()
             return c
@@ -154,8 +154,7 @@
                                      device_id=dev(a, oo), device_id_type=MESH).start()
         return c
     lax.fori_loop(0, 9, mo, 0)
-    for p in range(1, npair):
-        send_t1(p, 0, NT8)
+    send_t1(1, 0, NT8)
     mq[a] = mloc[...]
     pltpu.make_async_copy(mq.at[pl.ds(0, 3), pl.ds(0, 3)], mq.at[pl.ds(0, 3), pl.ds(0, 3)], morecv).wait()
     for b in range(4):
@@ -186,6 +185,8 @@
 
     def fit(p):
         pltpu.make_async_copy(rbuf.at[:, p], rbuf.at[:, p], trecv.at[p]).wait()
+        if p + 2 < npair:
+            send_t1(p + 2, 0, NT8)
         for q in range(4):
             x = jnp.concatenate([rbuf[s, p, q].reshape(LANES, LANES) for s in range(4)], axis=1)
             z = dot(jnp.concatenate([x, x, x], axis=1), msp[...].reshape(3 * 512, 512), NN)

time: 88.2 us -> 94.3 us (1.069)
  Pallas kernels: 86.4 us -> 92.5 us
    pallas_call x1, Pallas kernels: 86.4 us -> 92.5 us  [local_fock(): pl.pallas_call(lambda *refs: kernel(nm, nl, nq, nd, ni, *refs), out_shape...]
where the time goes in v3:
time: 94.3 us; the launch traced here: 94.1 us
  Pallas kernels  92.5 us (98%)
  local copies, waits for them, and re-layouts  1.65 us (2%)
    pallas_call x1, Pallas kernels, local_fock(): pl.pallas_call(lambda *refs: kernel(nm, nl, nq, nd, ni, *refs), out_shape...  92.5 us

profile of v3, /device:TPU:0, one launch (start us, length us, event | category | flops | bytes accessed | tf_op | source)
XLA Modules:
  0.0 94.1 jit_solution(11755112580957683306)
XLA Ops:
  0.0 92.5 %shard_map.37 = f32[58,8,58]{2,1,0:T(8,128)} custom-call(f32[58,232,116]{2,1,0:T(8,128)} %bitcast.6, f32[464,116]{1,0:T(8,128)} %bitcast.8, f32[160,232]{1,0:T(8,128)} %bitcast.9), custom_call_target="tpu_custom_call" | custom-call | tf_op jit(solution)/shard_map/pallas_call | solution.py:288
  92.5 1.6 %copy.5 = f32[8,58,58]{2,0,1:T(8,128)} copy(f32[8,58,58]{2,0,1:T(8,128)} %bitcast.7) | data formatting | bytes 215296

commit v4 on v3

--- a/solution.py
+++ b/solution.py
@@ -154,7 +154,8 @@
                                      device_id=dev(a, oo), device_id_type=MESH).start()
         return c
     lax.fori_loop(0, 9, mo, 0)
-    send_t1(1, 0, NT8)
+    for p in range(1, npair):
+        send_t1(p, 0, NT8)
     mq[a] = mloc[...]
     pltpu.make_async_copy(mq.at[pl.ds(0, 3), pl.ds(0, 3)], mq.at[pl.ds(0, 3), pl.ds(0, 3)], morecv).wait()
     for b in range(4):
@@ -185,8 +186,6 @@
 
     def fit(p):
         pltpu.make_async_copy(rbuf.at[:, p], rbuf.at[:, p], trecv.at[p]).wait()
-        if p + 2 < npair:
-            send_t1(p + 2, 0, NT8)
         for q in range(4):
             x = jnp.concatenate([rbuf[s, p, q].reshape(LANES, LANES) for s in range(4)], axis=1)
             z = dot(jnp.concatenate([x, x, x], axis=1), msp[...].reshape(3 * 512, 512), NN)

time: 94.3 us -> 87.7 us (0.930)
  Pallas kernels: 92.5 us -> 85.2 us
    pallas_call x1, Pallas kernels: 92.5 us -> 85.2 us  [local_fock(): pl.pallas_call(lambda *refs: kernel(nm, nl, nq, nd, ni, *refs), out_shape...]
where the time goes in v4:
time: 87.7 us; the launch traced here: 86.9 us
  Pallas kernels  85.2 us (97%)
  local copies, waits for them, and re-layouts  1.65 us (2%)
    pallas_call x1, Pallas kernels, local_fock(): pl.pallas_call(lambda *refs: kernel(nm, nl, nq, nd, ni, *refs), out_shape...  85.2 us

profile of v4, /device:TPU:0, one launch (start us, length us, event | category | flops | bytes accessed | tf_op | source)
XLA Modules:
  0.0 86.9 jit_solution(17348804289695656439)
XLA Ops:
  0.0 85.2 %shard_map.37 = f32[58,8,58]{2,1,0:T(8,128)} custom-call(f32[58,232,116]{2,1,0:T(8,128)} %bitcast.6, f32[464,116]{1,0:T(8,128)} %bitcast.8, f32[160,232]{1,0:T(8,128)} %bitcast.9), custom_call_target="tpu_custom_call" | custom-call | tf_op jit(solution)/shard_map/pallas_call | solution.py:287
  85.3 1.6 %copy.5 = f32[8,58,58]{2,0,1:T(8,128)} copy(f32[8,58,58]{2,0,1:T(8,128)} %bitcast.7) | data formatting | bytes 215296

commit v5 on v4

--- a/solution.py
+++ b/solution.py
@@ -12,7 +12,8 @@
 NT = (((1,), (1,)), ((), ()))
 LANES = 128
 MROW = 64
-NT8 = 8
+NT8 = 7
+PIECE = 12
 SP = 168
 
 
@@ -49,9 +50,9 @@
         return (sy, aa, oo)
 
     pltpu.make_async_copy(ct, cv, lsem.at[0]).start()
+    pltpu.make_async_copy(bt.at[pl.ds(8 * NT8, 2)], bv.at[pl.ds(8 * NT8, 2)], lsem.at[2]).start()
     for t in range(NT8):
-        n = min(8, nm - 8 * t)
-        pltpu.make_async_copy(bt.at[pl.ds(8 * t, n)], bv.at[pl.ds(8 * t, n)], bsem.at[t]).start()
+        pltpu.make_async_copy(bt.at[pl.ds(8 * t, 8)], bv.at[pl.ds(8 * t, 8)], bsem.at[t]).start()
         if t == 0:
             pltpu.make_async_copy(mt, mv, lsem.at[1]).start()
     barrier = pltpu.get_barrier_semaphore()
@@ -81,19 +82,37 @@
     gam = jnp.zeros((nd, LANES), F32)
     tr2 = tr
 
-    def tile(t, pairs, gam):
-        n = 2 * pairs
-        pltpu.make_async_copy(bt.at[pl.ds(0, n)], bv.at[pl.ds(0, n)], bsem.at[t]).wait()
+    lane = lax.broadcasted_iota(jnp.int32, (1, LANES), 1)
+    data = lane < nq
+
+    def tile(t, gam, tail, first):
+        pltpu.make_async_copy(bt.at[pl.ds(0, 8)], bv.at[pl.ds(0, 8)], bsem.at[t]).wait()
         cols = pltpu.roll(ctp[...], lax.rem(512 - (nm * o + 8 * t), 256), 1)
-        for r in range(0, n, 2):
-            x = jnp.concatenate([jnp.concatenate([bv[8 * t + r + e], jnp.zeros((nl, LANES - nq), F32)], axis=1) for e in range(2)], axis=1)
+        count = 0
+        if tail is not None:
+            count = min(8, 10 - first)
+            spare = jnp.concatenate([bv[8 * NT8 + tail], jnp.zeros((nl, LANES - nq), F32)], axis=1)
+            tcol = pltpu.roll(ctp[...], lax.rem(512 - (nm * o + 8 * NT8 + tail), 256), 1)[:, 0:1]
+        for r in range(0, 8, 2):
+            xs = []
+            for e in range(2):
+                x = jnp.concatenate([bv[8 * t + r + e], jnp.zeros((nl, LANES - nq), F32)], axis=1)
+                if r + e < count:
+                    x = jnp.where(data, x, pltpu.roll(spare, (nq - PIECE * (first + r + e)) % LANES, 1))
+                xs.append(x)
+            x = jnp.concatenate(xs, axis=1)
             x = jnp.concatenate([x, jnp.zeros((256 - nl, 2 * LANES), F32)], axis=0)
             y = dot(lhs, rhs6(split3(x), 0), NN)
             for e in range(2):
                 ye = y[:, e * LANES:(e + 1) * LANES]
                 tr2[pl.ds((r + e) * SP, nd * ni), :] = ye
-                w = ye * cols[:, r + e:r + e + 1]
-                gam = gam + w.reshape(ni, nd, LANES).sum(0)
+                col = cols[:, r + e:r + e + 1]
+                if r + e < count:
+                    w = (ye * jnp.where(data, col, tcol)).reshape(ni, nd, LANES).sum(0)
+                    moved = pltpu.roll(jnp.where(data, 0.0, w), (PIECE * (first + r + e) - nq) % LANES, 1)
+                    gam = gam + jnp.where(data, w, 0.0) + moved
+                else:
+                    gam = gam + (ye * col).reshape(ni, nd, LANES).sum(0)
         for g in range(16):
             d, h = g // 2, g % 2
             for p in range(npair):
@@ -126,15 +145,20 @@
             return c
         lax.fori_loop(0, 16, one, 0)
 
+    pltpu.make_async_copy(bt.at[pl.ds(0, 2)], bv.at[pl.ds(0, 2)], lsem.at[2]).wait()
+
     def two_tiles(u, gam):
-        gam = tile(2 * u, 4, gam)
-        gam = tile(2 * u + 1, 4, gam)
+        gam = tile(2 * u, gam, u, 0)
+        gam = tile(2 * u + 1, gam, u, 8)
         send_t1(0, 2 * u, 2)
         return gam
-    gam = lax.fori_loop(0, 3, two_tiles, gam)
-    gam = tile(6, 4, gam)
-    gam = tile(7, 1, gam)
-    send_t1(0, 6, 2)
+    gam = lax.fori_loop(0, 2, two_tiles, gam)
+
+    def one_tile(t, gam):
+        gam = tile(t, gam, None, 0)
+        send_t1(0, t, 1)
+        return gam
+    gam = lax.fori_loop(4, NT8, one_tile, gam)
 
     gsend[...] = gam
 
@@ -184,20 +208,52 @@
             jsend[aa, u] = jnp.where(low64, lo, hi)
         return c
 
+    row8 = lax.broadcasted_iota(jnp.int32, (8, LANES), 0)
+    lane8 = lax.broadcasted_iota(jnp.int32, (8, LANES), 1)
+    at0 = lane8 - PIECE * row8
+    at1 = lane8 - PIECE * (row8 + 8)
+    here0 = jnp.logical_and(at0 >= 0, at0 < PIECE)
+    here1 = jnp.logical_and(jnp.logical_and(at1 >= 0, at1 < PIECE), lane8 < nq)
+    zbuf[:, NT8] = jnp.zeros((4, 2, 8, 512), F32)
+
+    def tails(x):
+        f = [x[t].astype(F32) for t in range(4)]
+        out = []
+        for e in range(2):
+            for u in range(2):
+                v0 = pltpu.roll(f[2 * u][8 * e:8 * e + 8], LANES - nq, 1, stride=PIECE, stride_axis=0)
+                f1 = f[2 * u + 1][8 * e:8 * e + 8]
+                v1 = jnp.where(row8 == 0, pltpu.roll(f1, (8 * PIECE - nq) % LANES, 1), pltpu.roll(f1, (9 * PIECE - nq) % LANES, 1))
+                v = jnp.where(here0, v0, jnp.where(here1, v1, 0.0))
+                out.append(v.sum(0, keepdims=True))
+        return out
+
     def fit(p):
         pltpu.make_async_copy(rbuf.at[:, p], rbuf.at[:, p], trecv.at[p]).wait()
+        xs = []
+        for s in range(4):
+            rest = [w for q in range(4) for w in tails(rbuf[s, p, q, pl.ds(0, 4)])]
+            xs.append(jnp.concatenate([rbuf[s, p].reshape(4 * NT8 * 16, LANES), jnp.concatenate(rest, axis=0).astype(BF)], axis=0))
+        x = jnp.concatenate(xs, axis=1)
+        z = dot(jnp.concatenate([x, x, x], axis=1), msp[...].reshape(3 * 512, 512), NN)
+        main = 4 * NT8 * 16
+        zbuf[:, pl.ds(0, NT8)] = z[:main].reshape(4, NT8, 2, 8, 512)
         for q in range(4):
-            x = jnp.concatenate([rbuf[s, p, q].reshape(LANES, LANES) for s in range(4)], axis=1)
-            z = dot(jnp.concatenate([x, x, x], axis=1), msp[...].reshape(3 * 512, 512), NN)
-            zbuf[pl.ds(8 * q, 8)] = z.reshape(8, 2, 8, 512)
-        mid, low = own[0, p].reshape(LANES, LANES), own[1, p].reshape(LANES, LANES)
+            for e in range(2):
+                zbuf[q, NT8, e, pl.ds(0, 2)] = z[main + 4 * q + 2 * e:main + 4 * q + 2 * e + 2]
+        ml = []
+        for s in range(2):
+            rest = tails(own[s, p, pl.ds(0, 4)]) + [jnp.zeros((12, LANES), F32)]
+            ml.append(jnp.concatenate([own[s, p].reshape(NT8 * 16, LANES), jnp.concatenate(rest, axis=0).astype(BF)], axis=0))
+        mid, low = ml
         rows = pl.ds(pl.multiple_of(a * LANES, LANES), LANES)
         mh, mm = msp[0, rows], msp[1, rows]
         z = dot(jnp.concatenate([mid, mid, low], axis=1), jnp.concatenate([mh, mm, mh], axis=0), NN)
-        mine = pl.ds(8 * o, 8)
-        zbuf[mine] = zbuf[mine] + z.reshape(8, 2, 8, 512)
+        zbuf[o, pl.ds(0, NT8)] = zbuf[o, pl.ds(0, NT8)] + z[:NT8 * 16].reshape(NT8, 2, 8, 512)
         for e in range(2):
-            s3 = split3(zbuf[:, e].reshape(4 * MROW, 512))
+            zbuf[o, NT8, e, pl.ds(0, 2)] = zbuf[o, NT8, e, pl.ds(0, 2)] + z[NT8 * 16 + 2 * e:NT8 * 16 + 2 * e + 2]
+        for e in range(2):
+            s3 = split3(zbuf[:, :, e].reshape(4 * MROW, 512))
             k = dot(lhs6(s3, 1), rhs6(s3, 1), NT)
             if p == 0 and e == 0:
                 kacc[0] = k[:, :LANES]
@@ -294,9 +350,9 @@
                 V((8 * SP, LANES), F32), V((16, npair, NT8, 16, LANES), BF), V((4, npair, 4, NT8, 16, LANES), BF),
                 V((2, npair, NT8, 16, LANES), BF), V((4, LANES, LANES), F32), V((4, 4, LANES, LANES), F32), V((3, 512, 512), BF),
                 V((nd, LANES), F32), V((4, 4, nd, LANES), F32), V((4, nm // 2, nd, LANES), F32), V((4, nm // 2, nd, LANES), F32),
-                V((32, 2, 8, 512), F32), V((2, 256, LANES), F32), V((256, LANES), F32), V((256, LANES), F32), V((2, 4, 32, LANES), F32),
+                V((4, 8, 2, 8, 512), F32), V((2, 256, LANES), F32), V((256, LANES), F32), V((256, LANES), F32), V((2, 4, 32, LANES), F32),
                 V((8 * 32, LANES), F32), V((15, nd, LANES), F32),
-                dma((NT8,)), dma((2,)), dma, dma((npair,)), dma, dma, dma, dma, dma, dma, dma, dma, dma, dma, dma, dma],
+                dma((NT8,)), dma((3,)), dma, dma((npair,)), dma, dma, dma, dma, dma, dma, dma, dma, dma, dma, dma, dma],
             compiler_params=pltpu.CompilerParams(collective_id=0, has_side_effects=True, vmem_limit_bytes=60 * 2**20),
         )(bt, mt, ct)
         return jnp.transpose(g, (1, 0, 2))

time: 87.7 us -> 81.6 us (0.930)
  Pallas kernels: 85.2 us -> 79.8 us
    pallas_call x1, Pallas kernels: 85.2 us -> 79.8 us  [local_fock(): pl.pallas_call(lambda *refs: kernel(nm, nl, nq, nd, ni, *refs), out_shape...]
where the time goes in v5:
time: 81.6 us; the launch traced here: 81.4 us
  Pallas kernels  79.8 us (98%)
  local copies, waits for them, and re-layouts  1.65 us (2%)
    pallas_call x1, Pallas kernels, local_fock(): pl.pallas_call(lambda *refs: kernel(nm, nl, nq, nd, ni, *refs), out_shape...  79.8 us
    unnamed x1, local copies, waits for them, and re-layouts  1.65 us

profile of v5, /device:TPU:0, one launch (start us, length us, event | category | flops | bytes accessed | tf_op | source)
XLA Modules:
  0.0 81.4 jit_solution(13047550654236973323)
XLA Ops:
  0.0 79.8 %shard_map.37 = f32[58,8,58]{2,1,0:T(8,128)} custom-call(f32[58,232,116]{2,1,0:T(8,128)} %bitcast.6, f32[464,116]{1,0:T(8,128)} %bitcast.8, f32[160,232]{1,0:T(8,128)} %bitcast.9), custom_call_target="tpu_custom_call" | custom-call | tf_op jit(solution)/shard_map/pallas_call | solution.py:343
  79.8 1.6 %copy.5 = f32[8,58,58]{2,0,1:T(8,128)} copy(f32[8,58,58]{2,0,1:T(8,128)} %bitcast.7) | data formatting | bytes 215296

commit v6 on v5

--- a/solution.py
+++ b/solution.py
@@ -38,7 +38,7 @@
     return jnp.concatenate([h, m, h, m, l, h], axis=axis)
 
 
-def kernel(nm, nl, nq, nd, ni, bt, mt, ct, out, bv, mv, cv, ctp, tr, sbuf, rbuf, own, mloc, mq, msp, gsend, grecv, jsend, jrecv, zbuf, kacc, kin, kful, kmsg, krecv, gbuf,
+def kernel(nm, nl, nq, nd, ni, bt, mt, ct, out, bv, mv, cv, ctp, tr, sbuf, rbuf, own, mloc, mqr, mq, msp, gsend, grecv, jsend, jrecv, jfwd, zbuf, kacc, kin, kful, kmsg, krecv, gbuf,
            bsem, lsem, tsend, trecv, mzsend, mzrecv, mosend, morecv, gssem, grsem, jssem, jrsem, kxs, kxr, kss, krs):
     sy, a, o = lax.axis_index('sys'), lax.axis_index('aux'), lax.axis_index('orb')
     me = a * 4 + o
@@ -72,12 +72,29 @@
         mloc[b] = jnp.concatenate([blk, jnp.zeros((LANES - nq, LANES), F32)], axis=0)
     pl.semaphore_wait(barrier, 15)
 
-    def mz(j, c):
-        aa = lax.rem(a + j, 4)
-        pltpu.make_async_remote_copy(src_ref=mloc.at[o], dst_ref=mq.at[a, o], send_sem=mzsend, recv_sem=mzrecv,
-                                     device_id=dev(aa, o), device_id_type=MESH).start()
-        return c
-    lax.fori_loop(1, 4, mz, 0)
+    quarter = pl.ds(pl.multiple_of(o * 32, 32), 32)
+
+    def nearer(x, y, z):
+        dx, dy = jnp.abs(x - z), jnp.abs(y - z)
+        return jnp.logical_or(dx < dy, jnp.logical_and(dx == dy, x < y))
+
+    def metric_copies(act):
+        for k in (2, 1, 3):
+            to = lax.rem(a + 4 - k, 4)
+
+            def block(row, slot):
+                return pltpu.make_async_remote_copy(src_ref=mloc.at[row, quarter], dst_ref=mqr.at[slot, quarter], send_sem=mzsend,
+                                                    recv_sem=mzrecv, device_id=dev(to, o), device_id_type=MESH)
+            act(block(a, k - 1))
+            for k2 in (1, 2, 3):
+                if k2 == k:
+                    continue
+                b = lax.rem(to + k2, 4)
+
+                @pl.when(nearer(a, b, to))
+                def _():
+                    act(block(b, k + k2))
+    metric_copies(lambda c: c.start())
 
     gam = jnp.zeros((nd, LANES), F32)
     tr2 = tr
@@ -170,18 +187,31 @@
     lax.fori_loop(1, 16, gs, 0)
     pltpu.make_async_copy(gsend, grecv.at[a, o], grsem).start()
 
-    pltpu.make_async_copy(mq.at[pl.ds(0, 3), 0], mq.at[pl.ds(0, 3), 0], mzrecv).wait()
+    pltpu.make_async_copy(mqr.at[:, pl.ds(0, 32)], mqr.at[:, pl.ds(0, 32)], mzrecv).wait()
 
     def mo(k, c):
-        aa, oo = lax.rem(a + 1 + k // 3, 4), lax.rem(o + 1 + k % 3, 4)
-        pltpu.make_async_remote_copy(src_ref=mq.at[aa, o], dst_ref=mq.at[aa, o], send_sem=mosend, recv_sem=morecv,
+        oo = lax.rem(o + k, 4)
+        pltpu.make_async_remote_copy(src_ref=mqr.at[:, quarter], dst_ref=mqr.at[:, quarter], send_sem=mosend, recv_sem=morecv,
                                      device_id=dev(a, oo), device_id_type=MESH).start()
         return c
-    lax.fori_loop(0, 9, mo, 0)
-    for p in range(1, npair):
+    lax.fori_loop(1, 4, mo, 0)
+    for p in range(1, 3):
         send_t1(p, 0, NT8)
     mq[a] = mloc[...]
-    pltpu.make_async_copy(mq.at[pl.ds(0, 3), pl.ds(0, 3)], mq.at[pl.ds(0, 3), pl.ds(0, 3)], morecv).wait()
+    for k in range(1, 4):
+        c1 = lax.rem(a + k, 4)
+        mq[c1, a] = mloc[c1].T
+    pltpu.make_async_copy(mqr.at[:, pl.ds(0, 96)], mqr.at[:, pl.ds(0, 96)], morecv).wait()
+    for k in range(1, 4):
+        c1 = lax.rem(a + k, 4)
+        mq[c1, c1] = mqr[k - 1]
+        for k2 in range(k + 1, 4):
+            c2 = lax.rem(a + k2, 4)
+            first = jnp.where(nearer(c1, c2, a), c1, c2)
+            second = c1 + c2 - first
+            blk = mqr[k + k2]
+            mq[first, second] = blk
+            mq[second, first] = blk.T
     for b in range(4):
         parts = split3(jnp.concatenate([mq[aa, b] for aa in range(4)], axis=1))
         for s in range(3):
@@ -262,17 +292,23 @@
                 kacc[0] = kacc[0] + k[:, :LANES]
                 kacc[1] = kacc[1] + k[:, LANES:]
 
+    lax.fori_loop(0, nm // 2, jpair, 0)
+    near, far = a + 1 - 2 * (a % 2), lax.rem(a + 2, 4)
+    hops = []
+    for e, aa in enumerate((lax.rem(near + 2, 4), near)):
+        hops.append(pltpu.make_async_remote_copy(src_ref=jsend.at[aa], dst_ref=jrecv.at[e], send_sem=jssem.at[e], recv_sem=jrsem.at[e],
+                                                 device_id=dev(near, o), device_id_type=MESH))
+        hops[-1].start()
+    for p in range(3, npair):
+        send_t1(p, 0, NT8)
     fit(0)
-    lax.fori_loop(0, nm // 2, jpair, 0)
-
-    def js(j, c):
-        aa = lax.rem(a + j, 4)
-        pltpu.make_async_remote_copy(src_ref=jsend.at[aa], dst_ref=jrecv.at[a], send_sem=jssem, recv_sem=jrsem,
-                                     device_id=dev(aa, o), device_id_type=MESH).start()
-        return c
-    lax.fori_loop(1, 4, js, 0)
-    pltpu.make_async_copy(jsend.at[a], jrecv.at[a], jrsem).start()
-    for p in range(1, npair):
+    fit(1)
+    hops[0].wait_recv()
+    jfwd[...] = jsend[far] + jrecv[0]
+    cross = pltpu.make_async_remote_copy(src_ref=jfwd, dst_ref=jrecv.at[2], send_sem=jssem.at[2], recv_sem=jrsem.at[2],
+                                         device_id=dev(far, o), device_id_type=MESH)
+    cross.start()
+    for p in range(2, npair):
         fit(p)
 
     mate = o + 1 - 2 * half
@@ -305,19 +341,21 @@
         return c
     lax.fori_loop(0, 8, ks, 0)
 
-    pltpu.make_async_copy(jrecv, jrecv, jrsem).wait()
+    hops[1].wait_recv()
+    cross.wait_recv()
     pltpu.make_async_copy(krecv, krecv, krs).wait()
     for u in range(nm // 2):
-        j = jrecv[0, u] + jrecv[1, u] + jrecv[2, u] + jrecv[3, u]
+        j = jsend[a, u] + jrecv[1, u] + jrecv[2, u]
         g = 2.0 * j - krecv[pl.ds(u, nd, stride=32), :]
         out[2 * u] = g[:, :nm]
         out[2 * u + 1] = pltpu.roll(g, 64, 1)[:, :nm]
 
     pltpu.make_async_copy(sbuf.at[pl.ds(0, 15)], sbuf.at[pl.ds(0, 15)], tsend).wait()
-    pltpu.make_async_copy(mq.at[pl.ds(0, 3), 0], mq.at[pl.ds(0, 3), 0], mzsend).wait()
-    pltpu.make_async_copy(mq.at[pl.ds(0, 3), pl.ds(0, 3)], mq.at[pl.ds(0, 3), pl.ds(0, 3)], mosend).wait()
+    metric_copies(lambda c: c.wait_send())
+    pltpu.make_async_copy(mqr.at[:, pl.ds(0, 96)], mqr.at[:, pl.ds(0, 96)], mosend).wait()
     pltpu.make_async_copy(gbuf, gbuf, gssem).wait()
-    pltpu.make_async_copy(jsend.at[pl.ds(0, 3)], jsend.at[pl.ds(0, 3)], jssem).wait()
+    for c in hops + [cross]:
+        c.wait_send()
     swap.wait_send()
     inset = (a // 2) == half
 
@@ -348,11 +386,11 @@
             scratch_shapes=[
                 V((nm, nl, nq), F32), V((4 * nq, nq), F32), V((ni * nd, nl), F32), V((ni * nd, 256), F32),
                 V((8 * SP, LANES), F32), V((16, npair, NT8, 16, LANES), BF), V((4, npair, 4, NT8, 16, LANES), BF),
-                V((2, npair, NT8, 16, LANES), BF), V((4, LANES, LANES), F32), V((4, 4, LANES, LANES), F32), V((3, 512, 512), BF),
-                V((nd, LANES), F32), V((4, 4, nd, LANES), F32), V((4, nm // 2, nd, LANES), F32), V((4, nm // 2, nd, LANES), F32),
+                V((2, npair, NT8, 16, LANES), BF), V((4, LANES, LANES), F32), V((6, LANES, LANES), F32), V((4, 4, LANES, LANES), F32), V((3, 512, 512), BF),
+                V((nd, LANES), F32), V((4, 4, nd, LANES), F32), V((4, nm // 2, nd, LANES), F32), V((3, nm // 2, nd, LANES), F32), V((nm // 2, nd, LANES), F32),
                 V((4, 8, 2, 8, 512), F32), V((2, 256, LANES), F32), V((256, LANES), F32), V((256, LANES), F32), V((2, 4, 32, LANES), F32),
                 V((8 * 32, LANES), F32), V((15, nd, LANES), F32),
-                dma((NT8,)), dma((3,)), dma, dma((npair,)), dma, dma, dma, dma, dma, dma, dma, dma, dma, dma, dma, dma],
+                dma((NT8,)), dma((3,)), dma, dma((npair,)), dma, dma, dma, dma, dma, dma, dma((3,)), dma((3,)), dma, dma, dma, dma],
             compiler_params=pltpu.CompilerParams(collective_id=0, has_side_effects=True, vmem_limit_bytes=60 * 2**20),
         )(bt, mt, ct)
         return jnp.transpose(g, (1, 0, 2))

time: 81.6 us -> 75.5 us (0.925)
  Pallas kernels: 79.8 us -> 73.2 us
    pallas_call x1, Pallas kernels: 79.8 us -> 73.2 us  [local_fock(): pl.pallas_call(lambda *refs: kernel(nm, nl, nq, nd, ni, *refs), out_shape...]
where the time goes in v6:
time: 75.5 us; the launch traced here: 74.9 us
  Pallas kernels  73.2 us (97%)
  local copies, waits for them, and re-layouts  1.65 us (2%)
    pallas_call x1, Pallas kernels, local_fock(): pl.pallas_call(lambda *refs: kernel(nm, nl, nq, nd, ni, *refs), out_shape...  73.2 us
    unnamed x1, local copies, waits for them, and re-layouts  1.65 us

profile of v6, /device:TPU:0, one launch (start us, length us, event | category | flops | bytes accessed | tf_op | source)
XLA Modules:
  0.0 74.9 jit_solution(11436635361339393080)
XLA Ops:
  0.0 73.2 %shard_map.37 = f32[58,8,58]{2,1,0:T(8,128)} custom-call(f32[58,232,116]{2,1,0:T(8,128)} %bitcast.6, f32[464,116]{1,0:T(8,128)} %bitcast.8, f32[160,232]{1,0:T(8,128)} %bitcast.9), custom_call_target="tpu_custom_call" | custom-call | tf_op jit(solution)/shard_map/pallas_call | solution.py:381
  73.2 1.6 %copy.5 = f32[8,58,58]{2,0,1:T(8,128)} copy(f32[8,58,58]{2,0,1:T(8,128)} %bitcast.7) | data formatting | bytes 215296

commit v7 on v6

--- a/solution.py
+++ b/solution.py
@@ -142,38 +142,53 @@
             own[1, p, t] = low
         return gam
 
-    def send_t1(p, t0, nt):
+    outer = jnp.logical_or(a == 0, a == 3)
+    pair = a + 1 - 2 * (a % 2)
+
+    def send_t1(p, t0, nt, cross):
         def one(k, c):
-            j, u = k % 4, k // 4
-            aa = lax.rem(a + 2 + j, 4)
-            oo = lax.rem(o + 1 + u, 4)
+            if cross:
+                aa = jnp.where(k % 2 == 0, 3 - a, 3 - pair)
+                oo = lax.rem(o + 1 + k // 2, 4)
+            else:
+                aa = jnp.where(k % 2 == 0, pair, a)
+                oo = lax.rem(o + 1 + k // 2, 4)
             g = aa * 4 + oo
             src = sbuf.at[g, p, pl.ds(t0, nt)]
             dst = rbuf.at[a, p, o, pl.ds(t0, nt)]
 
-            @pl.when(k != 14)
-            def _():
+            def far():
                 pltpu.make_async_remote_copy(src_ref=src, dst_ref=dst, send_sem=tsend, recv_sem=trecv.at[p],
                                              device_id=dev(aa, oo), device_id_type=MESH).start()
-
-            @pl.when(k == 14)
-            def _():
-                pltpu.make_async_copy(src, dst, trecv.at[p]).start()
+            if cross:
+                far()
+            else:
+                pl.when(k != 7)(far)
+
+                @pl.when(k == 7)
+                def _():
+                    pltpu.make_async_copy(src, dst, trecv.at[p]).start()
             return c
-        lax.fori_loop(0, 16, one, 0)
+        lax.fori_loop(0, 8, one, 0)
+
+    def send_early(p, t0, nt):
+        @pl.when(jnp.logical_not(outer))
+        def _():
+            send_t1(p, t0, nt, True)
+        send_t1(p, t0, nt, False)
 
     pltpu.make_async_copy(bt.at[pl.ds(0, 2)], bv.at[pl.ds(0, 2)], lsem.at[2]).wait()
 
     def two_tiles(u, gam):
         gam = tile(2 * u, gam, u, 0)
         gam = tile(2 * u + 1, gam, u, 8)
-        send_t1(0, 2 * u, 2)
+        send_early(0, 2 * u, 2)
         return gam
     gam = lax.fori_loop(0, 2, two_tiles, gam)
 
     def one_tile(t, gam):
         gam = tile(t, gam, None, 0)
-        send_t1(0, t, 1)
+        send_early(0, t, 1)
         return gam
     gam = lax.fori_loop(4, NT8, one_tile, gam)
 
@@ -195,8 +210,8 @@
                                      device_id=dev(a, oo), device_id_type=MESH).start()
         return c
     lax.fori_loop(1, 4, mo, 0)
-    for p in range(1, 3):
-        send_t1(p, 0, NT8)
+    for p in range(1, npair):
+        send_early(p, 0, NT8)
     mq[a] = mloc[...]
     for k in range(1, 4):
         c1 = lax.rem(a + k, 4)
@@ -299,17 +314,18 @@
         hops.append(pltpu.make_async_remote_copy(src_ref=jsend.at[aa], dst_ref=jrecv.at[e], send_sem=jssem.at[e], recv_sem=jrsem.at[e],
                                                  device_id=dev(near, o), device_id_type=MESH))
         hops[-1].start()
-    for p in range(3, npair):
-        send_t1(p, 0, NT8)
-    fit(0)
-    fit(1)
+    @pl.when(outer)
+    def _():
+        for p in range(npair):
+            send_t1(p, 0, NT8, True)
+    for p in range(npair - 1):
+        fit(p)
     hops[0].wait_recv()
     jfwd[...] = jsend[far] + jrecv[0]
     cross = pltpu.make_async_remote_copy(src_ref=jfwd, dst_ref=jrecv.at[2], send_sem=jssem.at[2], recv_sem=jrsem.at[2],
                                          device_id=dev(far, o), device_id_type=MESH)
     cross.start()
-    for p in range(2, npair):
-        fit(p)
+    fit(npair - 1)
 
     mate = o + 1 - 2 * half
     swap = pltpu.make_async_remote_copy(src_ref=kacc.at[1 - half], dst_ref=kin, send_sem=kxs, recv_sem=kxr,

time: 75.5 us -> 79.7 us (1.056)
  Pallas kernels: 73.2 us -> 77.9 us
    pallas_call x1, Pallas kernels: 73.2 us -> 77.9 us  [local_fock(): pl.pallas_call(lambda *refs: kernel(nm, nl, nq, nd, ni, *refs), out_shape...]
where the time goes in v7:
time: 79.7 us; the launch traced here: 79.5 us
  Pallas kernels  77.9 us (98%)
  local copies, waits for them, and re-layouts  1.65 us (2%)
    pallas_call x1, Pallas kernels, local_fock(): pl.pallas_call(lambda *refs: kernel(nm, nl, nq, nd, ni, *refs), out_shape...  77.9 us
    unnamed x1, local copies, waits for them, and re-layouts  1.65 us

profile of v7, /device:TPU:0, one launch (start us, length us, event | category | flops | bytes accessed | tf_op | source)
XLA Modules:
  0.0 79.5 jit_solution(8118305291198588429)
XLA Ops:
  0.0 77.9 %shard_map.37 = f32[58,8,58]{2,1,0:T(8,128)} custom-call(f32[58,232,116]{2,1,0:T(8,128)} %bitcast.6, f32[464,116]{1,0:T(8,128)} %bitcast.8, f32[160,232]{1,0:T(8,128)} %bitcast.9), custom_call_target="tpu_custom_call" | custom-call | tf_op jit(solution)/shard_map/pallas_call | solution.py:397
  77.9 1.6 %copy.5 = f32[8,58,58]{2,0,1:T(8,128)} copy(f32[8,58,58]{2,0,1:T(8,128)} %bitcast.7) | data formatting | bytes 215296

commit v8 on v6

--- a/solution.py
+++ b/solution.py
@@ -142,14 +142,14 @@
             own[1, p, t] = low
         return gam
 
-    def send_t1(p, t0, nt):
+    def send_t1(p, t0, nt, np=1):
         def one(k, c):
             j, u = k % 4, k // 4
             aa = lax.rem(a + 2 + j, 4)
             oo = lax.rem(o + 1 + u, 4)
             g = aa * 4 + oo
-            src = sbuf.at[g, p, pl.ds(t0, nt)]
-            dst = rbuf.at[a, p, o, pl.ds(t0, nt)]
+            src = sbuf.at[g, pl.ds(p, np), pl.ds(t0, nt)]
+            dst = rbuf.at[a, o, pl.ds(p, np), pl.ds(t0, nt)]
 
             @pl.when(k != 14)
             def _():
@@ -166,16 +166,14 @@
 
     def two_tiles(u, gam):
         gam = tile(2 * u, gam, u, 0)
-        gam = tile(2 * u + 1, gam, u, 8)
-        send_t1(0, 2 * u, 2)
-        return gam
+        return tile(2 * u + 1, gam, u, 8)
     gam = lax.fori_loop(0, 2, two_tiles, gam)
+    send_t1(0, 0, 4)
 
     def one_tile(t, gam):
-        gam = tile(t, gam, None, 0)
-        send_t1(0, t, 1)
-        return gam
+        return tile(t, gam, None, 0)
     gam = lax.fori_loop(4, NT8, one_tile, gam)
+    send_t1(0, 4, 3)
 
     gsend[...] = gam
 
@@ -195,8 +193,7 @@
                                      device_id=dev(a, oo), device_id_type=MESH).start()
         return c
     lax.fori_loop(1, 4, mo, 0)
-    for p in range(1, 3):
-        send_t1(p, 0, NT8)
+    send_t1(1, 0, NT8, 2)
     mq[a] = mloc[...]
     for k in range(1, 4):
         c1 = lax.rem(a + k, 4)
@@ -259,11 +256,14 @@
         return out
 
     def fit(p):
-        pltpu.make_async_copy(rbuf.at[:, p], rbuf.at[:, p], trecv.at[p]).wait()
+        if p == 0:
+            pltpu.make_async_copy(rbuf.at[:, :, p], rbuf.at[:, :, p], trecv.at[p]).wait()
+        elif p % 2 == 1:
+            pltpu.make_async_copy(rbuf.at[:, :, pl.ds(p, 2)], rbuf.at[:, :, pl.ds(p, 2)], trecv.at[p]).wait()
         xs = []
         for s in range(4):
-            rest = [w for q in range(4) for w in tails(rbuf[s, p, q, pl.ds(0, 4)])]
-            xs.append(jnp.concatenate([rbuf[s, p].reshape(4 * NT8 * 16, LANES), jnp.concatenate(rest, axis=0).astype(BF)], axis=0))
+            rest = [w for q in range(4) for w in tails(rbuf[s, q, p, pl.ds(0, 4)])]
+            xs.append(jnp.concatenate([rbuf[s, :, p].reshape(4 * NT8 * 16, LANES), jnp.concatenate(rest, axis=0).astype(BF)], axis=0))
         x = jnp.concatenate(xs, axis=1)
         z = dot(jnp.concatenate([x, x, x], axis=1), msp[...].reshape(3 * 512, 512), NN)
         main = 4 * NT8 * 16
@@ -299,8 +299,7 @@
         hops.append(pltpu.make_async_remote_copy(src_ref=jsend.at[aa], dst_ref=jrecv.at[e], send_sem=jssem.at[e], recv_sem=jrsem.at[e],
                                                  device_id=dev(near, o), device_id_type=MESH))
         hops[-1].start()
-    for p in range(3, npair):
-        send_t1(p, 0, NT8)
+    send_t1(3, 0, NT8, 2)
     fit(0)
     fit(1)
     hops[0].wait_recv()
@@ -385,7 +384,7 @@
             out_specs=pl.BlockSpec(memory_space=pltpu.VMEM),
             scratch_shapes=[
                 V((nm, nl, nq), F32), V((4 * nq, nq), F32), V((ni * nd, nl), F32), V((ni * nd, 256), F32),
-                V((8 * SP, LANES), F32), V((16, npair, NT8, 16, LANES), BF), V((4, npair, 4, NT8, 16, LANES), BF),
+                V((8 * SP, LANES), F32), V((16, npair, NT8, 16, LANES), BF), V((4, 4, npair, NT8, 16, LANES), BF),
                 V((2, npair, NT8, 16, LANES), BF), V((4, LANES, LANES), F32), V((6, LANES, LANES), F32), V((4, 4, LANES, LANES), F32), V((3, 512, 512), BF),
                 V((nd, LANES), F32), V((4, 4, nd, LANES), F32), V((4, nm // 2, nd, LANES), F32), V((3, nm // 2, nd, LANES), F32), V((nm // 2, nd, LANES), F32),
                 V((4, 8, 2, 8, 512), F32), V((2, 256, LANES), F32), V((256, LANES), F32), V((256, LANES), F32), V((2, 4, 32, LANES), F32),

time: 75.5 us -> 79.5 us (1.053)
  Pallas kernels: 73.2 us -> 77.7 us
    pallas_call x1, Pallas kernels: 73.2 us -> 77.7 us  [local_fock(): pl.pallas_call(lambda *refs: kernel(nm, nl, nq, nd, ni, *refs), out_shape...]
where the time goes in v8:
time: 79.5 us; the launch traced here: 79.3 us
  Pallas kernels  77.7 us (98%)
  local copies, waits for them, and re-layouts  1.65 us (2%)
    pallas_call x1, Pallas kernels, local_fock(): pl.pallas_call(lambda *refs: kernel(nm, nl, nq, nd, ni, *refs), out_shape...  77.7 us
    unnamed x1, local copies, waits for them, and re-layouts  1.65 us

profile of v8, /device:TPU:0, one launch (start us, length us, event | category | flops | bytes accessed | tf_op | source)
XLA Modules:
  0.0 79.3 jit_solution(14411349435479499296)
XLA Ops:
  0.0 77.7 %shard_map.37 = f32[58,8,58]{2,1,0:T(8,128)} custom-call(f32[58,232,116]{2,1,0:T(8,128)} %bitcast.6, f32[464,116]{1,0:T(8,128)} %bitcast.8, f32[160,232]{1,0:T(8,128)} %bitcast.9), custom_call_target="tpu_custom_call" | custom-call | tf_op jit(solution)/shard_map/pallas_call | solution.py:380
  77.7 1.6 %copy.5 = f32[8,58,58]{2,0,1:T(8,128)} copy(f32[8,58,58]{2,0,1:T(8,128)} %bitcast.7) | data formatting | bytes 215296

commit v9 on v6

--- a/solution.py
+++ b/solution.py
@@ -166,8 +166,9 @@
 
     def two_tiles(u, gam):
         gam = tile(2 * u, gam, u, 0)
+        send_t1(0, 2 * u, 1)
         gam = tile(2 * u + 1, gam, u, 8)
-        send_t1(0, 2 * u, 2)
+        send_t1(0, 2 * u + 1, 1)
         return gam
     gam = lax.fori_loop(0, 2, two_tiles, gam)
 
@@ -301,15 +302,14 @@
         hops[-1].start()
     for p in range(3, npair):
         send_t1(p, 0, NT8)
-    fit(0)
-    fit(1)
+    for p in range(npair - 1):
+        fit(p)
     hops[0].wait_recv()
     jfwd[...] = jsend[far] + jrecv[0]
     cross = pltpu.make_async_remote_copy(src_ref=jfwd, dst_ref=jrecv.at[2], send_sem=jssem.at[2], recv_sem=jrsem.at[2],
                                          device_id=dev(far, o), device_id_type=MESH)
     cross.start()
-    for p in range(2, npair):
-        fit(p)
+    fit(npair - 1)
 
     mate = o + 1 - 2 * half
     swap = pltpu.make_async_remote_copy(src_ref=kacc.at[1 - half], dst_ref=kin, send_sem=kxs, recv_sem=kxr,

time: 75.5 us -> 75.6 us (level)
  no operation moved by 1% of the time
where the time goes in v9:
time: 75.6 us; the launch traced here: 75.5 us
  Pallas kernels  73.8 us (98%)
  local copies, waits for them, and re-layouts  1.65 us (2%)
    pallas_call x1, Pallas kernels, local_fock(): pl.pallas_call(lambda *refs: kernel(nm, nl, nq, nd, ni, *refs), out_shape...  73.8 us
    unnamed x1, local copies, waits for them, and re-layouts  1.65 us

profile of v9, /device:TPU:0, one launch (start us, length us, event | category | flops | bytes accessed | tf_op | source)
XLA Modules:
  0.0 75.5 jit_solution(4365198286041655919)
XLA Ops:
  0.0 73.8 %shard_map.37 = f32[58,8,58]{2,1,0:T(8,128)} custom-call(f32[58,232,116]{2,1,0:T(8,128)} %bitcast.6, f32[464,116]{1,0:T(8,128)} %bitcast.8, f32[160,232]{1,0:T(8,128)} %bitcast.9), custom_call_target="tpu_custom_call" | custom-call | tf_op jit(solution)/shard_map/pallas_call | solution.py:381
  73.8 1.6 %copy.5 = f32[8,58,58]{2,0,1:T(8,128)} copy(f32[8,58,58]{2,0,1:T(8,128)} %bitcast.7) | data formatting | bytes 215296

commit v10 on v9

--- a/solution.py
+++ b/solution.py
@@ -162,6 +162,35 @@
             return c
         lax.fori_loop(0, 16, one, 0)
 
+    outer = jnp.logical_or(a == 0, a == 3)
+    pair = a + 1 - 2 * (a % 2)
+
+    def send_half(p, t0, nt, cross):
+        def one(k, c):
+            if cross:
+                aa = jnp.where(k % 2 == 0, 3 - a, 3 - pair)
+                oo = lax.rem(o + 1 + k // 2, 4)
+            else:
+                aa = jnp.where(k % 2 == 0, pair, a)
+                oo = lax.rem(o + 1 + k // 2, 4)
+            g = aa * 4 + oo
+            src = sbuf.at[g, p, pl.ds(t0, nt)]
+            dst = rbuf.at[a, p, o, pl.ds(t0, nt)]
+
+            def far():
+                pltpu.make_async_remote_copy(src_ref=src, dst_ref=dst, send_sem=tsend, recv_sem=trecv.at[p],
+                                             device_id=dev(aa, oo), device_id_type=MESH).start()
+            if cross:
+                far()
+            else:
+                pl.when(k != 7)(far)
+
+                @pl.when(k == 7)
+                def _():
+                    pltpu.make_async_copy(src, dst, trecv.at[p]).start()
+            return c
+        lax.fori_loop(0, 8, one, 0)
+
     pltpu.make_async_copy(bt.at[pl.ds(0, 2)], bv.at[pl.ds(0, 2)], lsem.at[2]).wait()
 
     def two_tiles(u, gam):
@@ -196,8 +225,17 @@
                                      device_id=dev(a, oo), device_id_type=MESH).start()
         return c
     lax.fori_loop(1, 4, mo, 0)
-    for p in range(1, 3):
-        send_t1(p, 0, NT8)
+    @pl.when(outer)
+    def _():
+        for p in range(1, npair):
+            send_half(p, 0, NT8, True)
+        for p in range(1, npair):
+            send_half(p, 0, NT8, False)
+
+    @pl.when(jnp.logical_not(outer))
+    def _():
+        for p in range(1, 3):
+            send_t1(p, 0, NT8)
     mq[a] = mloc[...]
     for k in range(1, 4):
         c1 = lax.rem(a + k, 4)
@@ -300,8 +338,10 @@
         hops.append(pltpu.make_async_remote_copy(src_ref=jsend.at[aa], dst_ref=jrecv.at[e], send_sem=jssem.at[e], recv_sem=jrsem.at[e],
                                                  device_id=dev(near, o), device_id_type=MESH))
         hops[-1].start()
-    for p in range(3, npair):
-        send_t1(p, 0, NT8)
+    @pl.when(jnp.logical_not(outer))
+    def _():
+        for p in range(3, npair):
+            send_t1(p, 0, NT8)
     for p in range(npair - 1):
         fit(p)
     hops[0].wait_recv()

time: 75.6 us -> 83.9 us (1.11)
  Pallas kernels: 73.8 us -> 82.1 us
    pallas_call x1, Pallas kernels: 73.8 us -> 82.1 us  [local_fock(): pl.pallas_call(lambda *refs: kernel(nm, nl, nq, nd, ni, *refs), out_shape...]
where the time goes in v10:
time: 83.9 us; the launch traced here: 83.8 us
  Pallas kernels  82.1 us (98%)
  local copies, waits for them, and re-layouts  1.65 us (2%)
    pallas_call x1, Pallas kernels, local_fock(): pl.pallas_call(lambda *refs: kernel(nm, nl, nq, nd, ni, *refs), out_shape...  82.1 us

profile of v10, /device:TPU:0, one launch (start us, length us, event | category | flops | bytes accessed | tf_op | source)
XLA Modules:
  0.0 83.8 jit_solution(9301710053809463832)
XLA Ops:
  0.0 82.1 %shard_map.37 = f32[58,8,58]{2,1,0:T(8,128)} custom-call(f32[58,232,116]{2,1,0:T(8,128)} %bitcast.6, f32[464,116]{1,0:T(8,128)} %bitcast.8, f32[160,232]{1,0:T(8,128)} %bitcast.9), custom_call_target="tpu_custom_call" | custom-call | tf_op jit(solution)/shard_map/pallas_call | solution.py:421
  82.1 1.6 %copy.5 = f32[8,58,58]{2,0,1:T(8,128)} copy(f32[8,58,58]{2,0,1:T(8,128)} %bitcast.7) | data formatting | bytes 215296

commit v11 on v10

--- a/solution.py
+++ b/solution.py
@@ -227,10 +227,12 @@
     lax.fori_loop(1, 4, mo, 0)
     @pl.when(outer)
     def _():
-        for p in range(1, npair):
-            send_half(p, 0, NT8, True)
-        for p in range(1, npair):
-            send_half(p, 0, NT8, False)
+        send_half(1, 0, NT8, False)
+        send_half(2, 0, NT8, False)
+        send_half(1, 0, NT8, True)
+        send_half(3, 0, NT8, False)
+        send_half(4, 0, NT8, False)
+        send_half(2, 0, NT8, True)
 
     @pl.when(jnp.logical_not(outer))
     def _():
@@ -338,6 +340,11 @@
         hops.append(pltpu.make_async_remote_copy(src_ref=jsend.at[aa], dst_ref=jrecv.at[e], send_sem=jssem.at[e], recv_sem=jrsem.at[e],
                                                  device_id=dev(near, o), device_id_type=MESH))
         hops[-1].start()
+    @pl.when(outer)
+    def _():
+        for p in range(3, npair):
+            send_half(p, 0, NT8, True)
+
     @pl.when(jnp.logical_not(outer))
     def _():
         for p in range(3, npair):

time: 83.9 us -> 72 us (0.86)
  Pallas kernels: 82.1 us -> 70.2 us
    pallas_call x1, Pallas kernels: 82.1 us -> 70.2 us  [local_fock(): pl.pallas_call(lambda *refs: kernel(nm, nl, nq, nd, ni, *refs), out_shape...]
where the time goes in v11:
time: 72 us; the launch traced here: 71.9 us
  Pallas kernels  70.2 us (98%)
  local copies, waits for them, and re-layouts  1.65 us (2%)
    pallas_call x1, Pallas kernels, local_fock(): pl.pallas_call(lambda *refs: kernel(nm, nl, nq, nd, ni, *refs), out_shape...  70.2 us
    unnamed x1, local copies, waits for them, and re-layouts  1.65 us

profile of v11, /device:TPU:0, one launch (start us, length us, event | category | flops | bytes accessed | tf_op | source)
XLA Modules:
  0.0 71.9 jit_solution(5460695608251756191)
XLA Ops:
  0.0 70.2 %shard_map.37 = f32[58,8,58]{2,1,0:T(8,128)} custom-call(f32[58,232,116]{2,1,0:T(8,128)} %bitcast.6, f32[464,116]{1,0:T(8,128)} %bitcast.8, f32[160,232]{1,0:T(8,128)} %bitcast.9), custom_call_target="tpu_custom_call" | custom-call | tf_op jit(solution)/shard_map/pallas_call | solution.py:428
  70.3 1.6 %copy.5 = f32[8,58,58]{2,0,1:T(8,128)} copy(f32[8,58,58]{2,0,1:T(8,128)} %bitcast.7) | data formatting | bytes 215296

commit v12 on v10

--- a/solution.py
+++ b/solution.py
@@ -228,9 +228,8 @@
     @pl.when(outer)
     def _():
         for p in range(1, npair):
-            send_half(p, 0, NT8, True)
-        for p in range(1, npair):
             send_half(p, 0, NT8, False)
+        send_half(1, 0, NT8, True)
 
     @pl.when(jnp.logical_not(outer))
     def _():
@@ -338,6 +337,11 @@
         hops.append(pltpu.make_async_remote_copy(src_ref=jsend.at[aa], dst_ref=jrecv.at[e], send_sem=jssem.at[e], recv_sem=jrsem.at[e],
                                                  device_id=dev(near, o), device_id_type=MESH))
         hops[-1].start()
+    @pl.when(outer)
+    def _():
+        for p in range(2, npair):
+            send_half(p, 0, NT8, True)
+
     @pl.when(jnp.logical_not(outer))
     def _():
         for p in range(3, npair):
@@ -420,7 +424,7 @@
         dma = pltpu.SemaphoreType.DMA
         g = pl.pallas_call(
             lambda *refs: kernel(nm, nl, nq, nd, ni, *refs),
-            out_shape=jax.ShapeDtypeStruct((nm, nd, nm), F32),
+            out_shape=pltpu.VMEM((nm, nd, nm), F32),
             in_specs=[pl.BlockSpec(memory_space=pl.ANY)] * 3,
             out_specs=pl.BlockSpec(memory_space=pltpu.VMEM),
             scratch_shapes=[

time: 83.9 us -> 75.5 us (0.90)
  Pallas kernels: 82.1 us -> 74.7 us
  local copies, waits for them, and re-layouts: 1.65 us -> 0.69 us
    pallas_call x1, Pallas kernels: 82.1 us -> 74.7 us  [local_fock(): pl.pallas_call(lambda *refs: kernel(nm, nl, nq, nd, ni, *refs), out_shape...]
    unnamed x1, local copies, waits for them, and re-layouts: 1.65 us -> 0.69 us
where the time goes in v12:
time: 75.5 us; the launch traced here: 75.4 us
  Pallas kernels  74.7 us (99%)
    pallas_call x1, Pallas kernels, local_fock(): pl.pallas_call(lambda *refs: kernel(nm, nl, nq, nd, ni, *refs), out_shape...  74.7 us

profile of v12, /device:TPU:0, one launch (start us, length us, event | category | flops | bytes accessed | tf_op | source)
XLA Modules:
  0.0 75.4 jit_solution(3762008179858810215)
XLA Ops:
  0.0 74.7 %shard_map.37 = f32[58,8,58]{2,1,0:T(8,128)S(1)} custom-call(f32[58,232,116]{2,1,0:T(8,128)} %bitcast.7, f32[464,116]{1,0:T(8,128)} %bitcast.8, f32[160,232]{1,0:T(8,128)} %bitcast.9), custom_call_target="tpu_custom_call" | custom-call | tf_op jit(solution)/shard_map/pallas_call | solution.py:425
  74.7 0.7 copy.5

commit v13 on v11

--- a/solution.py
+++ b/solution.py
@@ -301,6 +301,10 @@
 
     def fit(p):
         pltpu.make_async_copy(rbuf.at[:, p], rbuf.at[:, p], trecv.at[p]).wait()
+        if p + 3 < npair:
+            @pl.when(jnp.logical_not(outer))
+            def _():
+                send_half(p + 3, 0, NT8, True)
         xs = []
         for s in range(4):
             rest = [w for q in range(4) for w in tails(rbuf[s, p, q, pl.ds(0, 4)])]
@@ -348,7 +352,7 @@
     @pl.when(jnp.logical_not(outer))
     def _():
         for p in range(3, npair):
-            send_t1(p, 0, NT8)
+            send_half(p, 0, NT8, False)
     for p in range(npair - 1):
         fit(p)
     hops[0].wait_recv()
@@ -427,7 +431,7 @@
         dma = pltpu.SemaphoreType.DMA
         g = pl.pallas_call(
             lambda *refs: kernel(nm, nl, nq, nd, ni, *refs),
-            out_shape=jax.ShapeDtypeStruct((nm, nd, nm), F32),
+            out_shape=pltpu.VMEM((nm, nd, nm), F32),
             in_specs=[pl.BlockSpec(memory_space=pl.ANY)] * 3,
             out_specs=pl.BlockSpec(memory_space=pltpu.VMEM),
             scratch_shapes=[

time: 72 us -> 70.7 us (0.982)
  local copies, waits for them, and re-layouts: 1.65 us -> 0.69 us
    unnamed x1, local copies, waits for them, and re-layouts: 1.65 us -> 0.69 us
where the time goes in v13:
time: 70.7 us; the launch traced here: 70.5 us
  Pallas kernels  69.8 us (99%)
    pallas_call x1, Pallas kernels, local_fock(): pl.pallas_call(lambda *refs: kernel(nm, nl, nq, nd, ni, *refs), out_shape...  69.8 us

profile of v13, /device:TPU:0, one launch (start us, length us, event | category | flops | bytes accessed | tf_op | source)
XLA Modules:
  0.0 70.5 jit_solution(1346575368143602182)
XLA Ops:
  0.0 69.8 %shard_map.37 = f32[58,8,58]{2,1,0:T(8,128)S(1)} custom-call(f32[58,232,116]{2,1,0:T(8,128)} %bitcast.7, f32[464,116]{1,0:T(8,128)} %bitcast.8, f32[160,232]{1,0:T(8,128)} %bitcast.9), custom_call_target="tpu_custom_call" | custom-call | tf_op jit(solution)/shard_map/pallas_call | solution.py:432
  69.8 0.7 copy.5

commit v14 on v13

--- a/solution.py
+++ b/solution.py
@@ -49,12 +49,11 @@
     def dev(aa, oo):
         return (sy, aa, oo)
 
+    pltpu.make_async_copy(mt, mv, lsem.at[1]).start()
     pltpu.make_async_copy(ct, cv, lsem.at[0]).start()
     pltpu.make_async_copy(bt.at[pl.ds(8 * NT8, 2)], bv.at[pl.ds(8 * NT8, 2)], lsem.at[2]).start()
     for t in range(NT8):
         pltpu.make_async_copy(bt.at[pl.ds(8 * t, 8)], bv.at[pl.ds(8 * t, 8)], bsem.at[t]).start()
-        if t == 0:
-            pltpu.make_async_copy(mt, mv, lsem.at[1]).start()
     barrier = pltpu.get_barrier_semaphore()
 
     def tell(k, c):
@@ -63,9 +62,6 @@
         return c
     lax.fori_loop(1, 16, tell, 0)
 
-    pltpu.make_async_copy(ct, cv, lsem.at[0]).wait()
-    ctp[...] = jnp.concatenate([cv[...], jnp.zeros((nd * ni, 256 - nl), F32)], axis=1)
-    lhs = lhs6(split3(ctp[...]), 1)
     pltpu.make_async_copy(mt, mv, lsem.at[1]).wait()
     for b in range(4):
         blk = jnp.concatenate([mv[nq * b:nq * (b + 1), :], jnp.zeros((nq, LANES - nq), F32)], axis=1)
@@ -95,6 +91,10 @@
                 def _():
                     act(block(b, k + k2))
     metric_copies(lambda c: c.start())
+
+    pltpu.make_async_copy(ct, cv, lsem.at[0]).wait()
+    ctp[...] = jnp.concatenate([cv[...], jnp.zeros((nd * ni, 256 - nl), F32)], axis=1)
+    lhs = lhs6(split3(ctp[...]), 1)
 
     gam = jnp.zeros((nd, LANES), F32)
     tr2 = tr
@@ -338,12 +338,22 @@
                 kacc[1] = kacc[1] + k[:, LANES:]
 
     lax.fori_loop(0, nm // 2, jpair, 0)
-    near, far = a + 1 - 2 * (a % 2), lax.rem(a + 2, 4)
-    hops = []
-    for e, aa in enumerate((lax.rem(near + 2, 4), near)):
-        hops.append(pltpu.make_async_remote_copy(src_ref=jsend.at[aa], dst_ref=jrecv.at[e], send_sem=jssem.at[e], recv_sem=jrsem.at[e],
-                                                 device_id=dev(near, o), device_id_type=MESH))
-        hops[-1].start()
+    inner = jnp.logical_not(outer)
+    fars = (3 - pair, 3 - a)
+
+    def jhop(aa, e):
+        return pltpu.make_async_remote_copy(src_ref=jsend.at[aa], dst_ref=jrecv.at[e], send_sem=jssem.at[e], recv_sem=jrsem.at[e],
+                                            device_id=dev(pair, o), device_id_type=MESH)
+
+    def jcross(e):
+        return pltpu.make_async_remote_copy(src_ref=jfwd.at[e], dst_ref=jrecv.at[3], send_sem=jssem.at[3 + e], recv_sem=jrsem.at[3],
+                                            device_id=dev(fars[e], o), device_id_type=MESH)
+
+    @pl.when(outer)
+    def _():
+        jhop(3 - a, 0).start()
+        jhop(3 - pair, 1).start()
+    jhop(pair, 2).start()
     @pl.when(outer)
     def _():
         for p in range(3, npair):
@@ -353,14 +363,17 @@
     def _():
         for p in range(3, npair):
             send_half(p, 0, NT8, False)
-    for p in range(npair - 1):
+    for p in range(3):
         fit(p)
-    hops[0].wait_recv()
-    jfwd[...] = jsend[far] + jrecv[0]
-    cross = pltpu.make_async_remote_copy(src_ref=jfwd, dst_ref=jrecv.at[2], send_sem=jssem.at[2], recv_sem=jrsem.at[2],
-                                         device_id=dev(far, o), device_id_type=MESH)
-    cross.start()
-    fit(npair - 1)
+
+    @pl.when(inner)
+    def _():
+        for e in range(2):
+            jhop(pair, e).wait_recv()
+            jfwd[e] = jsend[fars[e]] + jrecv[e]
+            jcross(e).start()
+    for p in range(3, npair):
+        fit(p)
 
     mate = o + 1 - 2 * half
     swap = pltpu.make_async_remote_copy(src_ref=kacc.at[1 - half], dst_ref=kin, send_sem=kxs, recv_sem=kxr,
@@ -392,11 +405,11 @@
         return c
     lax.fori_loop(0, 8, ks, 0)
 
-    hops[1].wait_recv()
-    cross.wait_recv()
+    jhop(pair, 2).wait_recv()
+    jcross(0).wait_recv()
     pltpu.make_async_copy(krecv, krecv, krs).wait()
     for u in range(nm // 2):
-        j = jsend[a, u] + jrecv[1, u] + jrecv[2, u]
+        j = jsend[a, u] + jrecv[2, u] + jrecv[3, u]
         g = 2.0 * j - krecv[pl.ds(u, nd, stride=32), :]
         out[2 * u] = g[:, :nm]
         out[2 * u + 1] = pltpu.roll(g, 64, 1)[:, :nm]
@@ -405,8 +418,17 @@
     metric_copies(lambda c: c.wait_send())
     pltpu.make_async_copy(mqr.at[:, pl.ds(0, 96)], mqr.at[:, pl.ds(0, 96)], mosend).wait()
     pltpu.make_async_copy(gbuf, gbuf, gssem).wait()
-    for c in hops + [cross]:
-        c.wait_send()
+    jhop(pair, 2).wait_send()
+
+    @pl.when(outer)
+    def _():
+        jhop(3 - a, 0).wait_send()
+        jhop(3 - pair, 1).wait_send()
+
+    @pl.when(inner)
+    def _():
+        jcross(0).wait_send()
+        jcross(1).wait_send()
     swap.wait_send()
     inset = (a // 2) == half
 
@@ -438,10 +460,10 @@
                 V((nm, nl, nq), F32), V((4 * nq, nq), F32), V((ni * nd, nl), F32), V((ni * nd, 256), F32),
                 V((8 * SP, LANES), F32), V((16, npair, NT8, 16, LANES), BF), V((4, npair, 4, NT8, 16, LANES), BF),
                 V((2, npair, NT8, 16, LANES), BF), V((4, LANES, LANES), F32), V((6, LANES, LANES), F32), V((4, 4, LANES, LANES), F32), V((3, 512, 512), BF),
-                V((nd, LANES), F32), V((4, 4, nd, LANES), F32), V((4, nm // 2, nd, LANES), F32), V((3, nm // 2, nd, LANES), F32), V((nm // 2, nd, LANES), F32),
+                V((nd, LANES), F32), V((4, 4, nd, LANES), F32), V((4, nm // 2, nd, LANES), F32), V((4, nm // 2, nd, LANES), F32), V((2, nm // 2, nd, LANES), F32),
                 V((4, 8, 2, 8, 512), F32), V((2, 256, LANES), F32), V((256, LANES), F32), V((256, LANES), F32), V((2, 4, 32, LANES), F32),
                 V((8 * 32, LANES), F32), V((15, nd, LANES), F32),
-                dma((NT8,)), dma((3,)), dma, dma((npair,)), dma, dma, dma, dma, dma, dma, dma((3,)), dma((3,)), dma, dma, dma, dma],
+                dma((NT8,)), dma((3,)), dma, dma((npair,)), dma, dma, dma, dma, dma, dma, dma((5,)), dma((4,)), dma, dma, dma, dma],
             compiler_params=pltpu.CompilerParams(collective_id=0, has_side_effects=True, vmem_limit_bytes=60 * 2**20),
         )(bt, mt, ct)
         return jnp.transpose(g, (1, 0, 2))

time: 70.7 us -> 72.5 us (1.025)
  Pallas kernels: 69.8 us -> 71.6 us
    pallas_call x1, Pallas kernels: 69.8 us -> 71.6 us  [local_fock(): pl.pallas_call(lambda *refs: kernel(nm, nl, nq, nd, ni, *refs), out_shape...]
where the time goes in v14:
time: 72.5 us; the launch traced here: 72.3 us
  Pallas kernels  71.6 us (99%)
    pallas_call x1, Pallas kernels, local_fock(): pl.pallas_call(lambda *refs: kernel(nm, nl, nq, nd, ni, *refs), out_shape...  71.6 us

profile of v14, /device:TPU:0, one launch (start us, length us, event | category | flops | bytes accessed | tf_op | source)
XLA Modules:
  0.0 72.3 jit_solution(16793236947316418974)
XLA Ops:
  0.0 71.6 %shard_map.37 = f32[58,8,58]{2,1,0:T(8,128)S(1)} custom-call(f32[58,232,116]{2,1,0:T(8,128)} %bitcast.7, f32[464,116]{1,0:T(8,128)} %bitcast.8, f32[160,232]{1,0:T(8,128)} %bitcast.9), custom_call_target="tpu_custom_call" | custom-call | tf_op jit(solution)/shard_map/pallas_call | solution.py:454
  71.6 0.7 copy.5

commit v15 on v13

--- a/solution.py
+++ b/solution.py
@@ -49,12 +49,11 @@
     def dev(aa, oo):
         return (sy, aa, oo)
 
+    pltpu.make_async_copy(mt, mv, lsem.at[1]).start()
     pltpu.make_async_copy(ct, cv, lsem.at[0]).start()
     pltpu.make_async_copy(bt.at[pl.ds(8 * NT8, 2)], bv.at[pl.ds(8 * NT8, 2)], lsem.at[2]).start()
     for t in range(NT8):
         pltpu.make_async_copy(bt.at[pl.ds(8 * t, 8)], bv.at[pl.ds(8 * t, 8)], bsem.at[t]).start()
-        if t == 0:
-            pltpu.make_async_copy(mt, mv, lsem.at[1]).start()
     barrier = pltpu.get_barrier_semaphore()
 
     def tell(k, c):
@@ -63,9 +62,6 @@
         return c
     lax.fori_loop(1, 16, tell, 0)
 
-    pltpu.make_async_copy(ct, cv, lsem.at[0]).wait()
-    ctp[...] = jnp.concatenate([cv[...], jnp.zeros((nd * ni, 256 - nl), F32)], axis=1)
-    lhs = lhs6(split3(ctp[...]), 1)
     pltpu.make_async_copy(mt, mv, lsem.at[1]).wait()
     for b in range(4):
         blk = jnp.concatenate([mv[nq * b:nq * (b + 1), :], jnp.zeros((nq, LANES - nq), F32)], axis=1)
@@ -95,6 +91,10 @@
                 def _():
                     act(block(b, k + k2))
     metric_copies(lambda c: c.start())
+
+    pltpu.make_async_copy(ct, cv, lsem.at[0]).wait()
+    ctp[...] = jnp.concatenate([cv[...], jnp.zeros((nd * ni, 256 - nl), F32)], axis=1)
+    lhs = lhs6(split3(ctp[...]), 1)
 
     gam = jnp.zeros((nd, LANES), F32)
     tr2 = tr
@@ -236,8 +236,8 @@
 
     @pl.when(jnp.logical_not(outer))
     def _():
-        for p in range(1, 3):
-            send_t1(p, 0, NT8)
+        send_t1(1, 0, NT8)
+        send_half(2, 0, NT8, False)
     mq[a] = mloc[...]
     for k in range(1, 4):
         c1 = lax.rem(a + k, 4)
@@ -301,10 +301,10 @@
 
     def fit(p):
         pltpu.make_async_copy(rbuf.at[:, p], rbuf.at[:, p], trecv.at[p]).wait()
-        if p + 3 < npair:
+        if p + 2 < npair:
             @pl.when(jnp.logical_not(outer))
             def _():
-                send_half(p + 3, 0, NT8, True)
+                send_half(p + 2, 0, NT8, True)
         xs = []
         for s in range(4):
             rest = [w for q in range(4) for w in tails(rbuf[s, p, q, pl.ds(0, 4)])]

time: 70.7 us -> 75.7 us (1.071)
  Pallas kernels: 69.8 us -> 74.8 us
    pallas_call x1, Pallas kernels: 69.8 us -> 74.8 us  [local_fock(): pl.pallas_call(lambda *refs: kernel(nm, nl, nq, nd, ni, *refs), out_shape...]
where the time goes in v15:
time: 75.7 us; the launch traced here: 75.5 us
  Pallas kernels  74.8 us (99%)
    pallas_call x1, Pallas kernels, local_fock(): pl.pallas_call(lambda *refs: kernel(nm, nl, nq, nd, ni, *refs), out_shape...  74.8 us

profile of v15, /device:TPU:0, one launch (start us, length us, event | category | flops | bytes accessed | tf_op | source)
XLA Modules:
  0.0 75.5 jit_solution(15371967826431204600)
XLA Ops:
  0.0 74.8 %shard_map.37 = f32[58,8,58]{2,1,0:T(8,128)S(1)} custom-call(f32[58,232,116]{2,1,0:T(8,128)} %bitcast.7, f32[464,116]{1,0:T(8,128)} %bitcast.8, f32[160,232]{1,0:T(8,128)} %bitcast.9), custom_call_target="tpu_custom_call" | custom-call | tf_op jit(solution)/shard_map/pallas_call | solution.py:432
  74.8 0.7 copy.5

commit v16 on v13

--- a/solution.py
+++ b/solution.py
@@ -233,6 +233,7 @@
         send_half(3, 0, NT8, False)
         send_half(4, 0, NT8, False)
         send_half(2, 0, NT8, True)
+        send_half(3, 0, NT8, True)
 
     @pl.when(jnp.logical_not(outer))
     def _():
@@ -346,8 +347,7 @@
         hops[-1].start()
     @pl.when(outer)
     def _():
-        for p in range(3, npair):
-            send_half(p, 0, NT8, True)
+        send_half(npair - 1, 0, NT8, True)
 
     @pl.when(jnp.logical_not(outer))
     def _():

time: 70.7 us -> 70.6 us (level)
  no operation moved by 1% of the time
where the time goes in v16:
time: 70.6 us; the launch traced here: 70.5 us
  Pallas kernels  69.7 us (99%)
    pallas_call x1, Pallas kernels, local_fock(): pl.pallas_call(lambda *refs: kernel(nm, nl, nq, nd, ni, *refs), out_shape...  69.7 us

profile of v16, /device:TPU:0, one launch (start us, length us, event | category | flops | bytes accessed | tf_op | source)
XLA Modules:
  0.0 70.5 jit_solution(4500613406162342985)
XLA Ops:
  0.0 69.7 %shard_map.37 = f32[58,8,58]{2,1,0:T(8,128)S(1)} custom-call(f32[58,232,116]{2,1,0:T(8,128)} %bitcast.7, f32[464,116]{1,0:T(8,128)} %bitcast.8, f32[160,232]{1,0:T(8,128)} %bitcast.9), custom_call_target="tpu_custom_call" | custom-call | tf_op jit(solution)/shard_map/pallas_call | solution.py:432
  69.8 0.7 copy.5

commit v17 on v9

--- a/solution.py
+++ b/solution.py
@@ -39,7 +39,7 @@
 
 
 def kernel(nm, nl, nq, nd, ni, bt, mt, ct, out, bv, mv, cv, ctp, tr, sbuf, rbuf, own, mloc, mqr, mq, msp, gsend, grecv, jsend, jrecv, jfwd, zbuf, kacc, kin, kful, kmsg, krecv, gbuf,
-           bsem, lsem, tsend, trecv, mzsend, mzrecv, mosend, morecv, gssem, grsem, jssem, jrsem, kxs, kxr, kss, krs):
+           bsem, lsem, tsend, nrecv, trecv, mzsend, mzrecv, mosend, morecv, gssem, grsem, jssem, jrsem, kxs, kxr, kss, krs):
     sy, a, o = lax.axis_index('sys'), lax.axis_index('aux'), lax.axis_index('orb')
     me = a * 4 + o
     dens, half = me // 2, me % 2
@@ -142,39 +142,52 @@
             own[1, p, t] = low
         return gam
 
-    def send_t1(p, t0, nt):
+    outer = jnp.logical_or(a == 0, a == 3)
+    pair = a + 1 - 2 * (a % 2)
+
+    def send_cross(p, t0, nt):
         def one(k, c):
-            j, u = k % 4, k // 4
-            aa = lax.rem(a + 2 + j, 4)
-            oo = lax.rem(o + 1 + u, 4)
-            g = aa * 4 + oo
-            src = sbuf.at[g, p, pl.ds(t0, nt)]
-            dst = rbuf.at[a, p, o, pl.ds(t0, nt)]
-
-            @pl.when(k != 14)
+            aa = jnp.where(k % 2 == 0, 3 - a, 3 - pair)
+            oo = lax.rem(o + 1 + k // 2, 4)
+            pltpu.make_async_remote_copy(src_ref=sbuf.at[aa * 4 + oo, p, pl.ds(t0, nt)], dst_ref=rbuf.at[a, p, o, pl.ds(t0, nt)],
+                                         send_sem=tsend, recv_sem=trecv.at[p], device_id=dev(aa, oo), device_id_type=MESH).start()
+            return c
+        lax.fori_loop(0, 8, one, 0)
+
+    def send_near(t):
+        def one(k, c):
+            aa = jnp.where(k % 2 == 0, pair, a)
+            oo = lax.rem(o + 1 + k // 2, 4)
+            src = sbuf.at[aa * 4 + oo, :, t]
+            dst = rbuf.at[a, :, o, t]
+
+            @pl.when(k != 7)
             def _():
-                pltpu.make_async_remote_copy(src_ref=src, dst_ref=dst, send_sem=tsend, recv_sem=trecv.at[p],
+                pltpu.make_async_remote_copy(src_ref=src, dst_ref=dst, send_sem=tsend, recv_sem=nrecv,
                                              device_id=dev(aa, oo), device_id_type=MESH).start()
 
-            @pl.when(k == 14)
+            @pl.when(k == 7)
             def _():
-                pltpu.make_async_copy(src, dst, trecv.at[p]).start()
+                pltpu.make_async_copy(src, dst, nrecv).start()
             return c
-        lax.fori_loop(0, 16, one, 0)
+        lax.fori_loop(0, 8, one, 0)
 
     pltpu.make_async_copy(bt.at[pl.ds(0, 2)], bv.at[pl.ds(0, 2)], lsem.at[2]).wait()
 
     def two_tiles(u, gam):
         gam = tile(2 * u, gam, u, 0)
-        send_t1(0, 2 * u, 1)
+        send_cross(0, 2 * u, 1)
+        send_near(2 * u)
         gam = tile(2 * u + 1, gam, u, 8)
-        send_t1(0, 2 * u + 1, 1)
+        send_cross(0, 2 * u + 1, 1)
+        send_near(2 * u + 1)
         return gam
     gam = lax.fori_loop(0, 2, two_tiles, gam)
 
     def one_tile(t, gam):
         gam = tile(t, gam, None, 0)
-        send_t1(0, t, 1)
+        send_cross(0, t, 1)
+        send_near(t)
         return gam
     gam = lax.fori_loop(4, NT8, one_tile, gam)
 
@@ -196,8 +209,12 @@
                                      device_id=dev(a, oo), device_id_type=MESH).start()
         return c
     lax.fori_loop(1, 4, mo, 0)
-    for p in range(1, 3):
-        send_t1(p, 0, NT8)
+    send_cross(1, 0, NT8)
+    send_cross(2, 0, NT8)
+
+    @pl.when(outer)
+    def _():
+        send_cross(3, 0, NT8)
     mq[a] = mloc[...]
     for k in range(1, 4):
         c1 = lax.rem(a + k, 4)
@@ -260,7 +277,11 @@
         return out
 
     def fit(p):
-        pltpu.make_async_copy(rbuf.at[:, p], rbuf.at[:, p], trecv.at[p]).wait()
+        pltpu.make_async_copy(rbuf.at[pl.ds(0, 2), p], rbuf.at[pl.ds(0, 2), p], trecv.at[p]).wait()
+        if p + 3 < npair:
+            @pl.when(jnp.logical_not(outer))
+            def _():
+                send_cross(p + 3, 0, NT8)
         xs = []
         for s in range(4):
             rest = [w for q in range(4) for w in tails(rbuf[s, p, q, pl.ds(0, 4)])]
@@ -300,8 +321,10 @@
         hops.append(pltpu.make_async_remote_copy(src_ref=jsend.at[aa], dst_ref=jrecv.at[e], send_sem=jssem.at[e], recv_sem=jrsem.at[e],
                                                  device_id=dev(near, o), device_id_type=MESH))
         hops[-1].start()
-    for p in range(3, npair):
-        send_t1(p, 0, NT8)
+    @pl.when(outer)
+    def _():
+        send_cross(npair - 1, 0, NT8)
+    pltpu.make_async_copy(rbuf.at[pl.ds(0, 2)], rbuf.at[pl.ds(0, 2)], nrecv).wait()
     for p in range(npair - 1):
         fit(p)
     hops[0].wait_recv()
@@ -380,7 +403,7 @@
         dma = pltpu.SemaphoreType.DMA
         g = pl.pallas_call(
             lambda *refs: kernel(nm, nl, nq, nd, ni, *refs),
-            out_shape=jax.ShapeDtypeStruct((nm, nd, nm), F32),
+            out_shape=pltpu.VMEM((nm, nd, nm), F32),
             in_specs=[pl.BlockSpec(memory_space=pl.ANY)] * 3,
             out_specs=pl.BlockSpec(memory_space=pltpu.VMEM),
             scratch_shapes=[
@@ -390,7 +413,7 @@
                 V((nd, LANES), F32), V((4, 4, nd, LANES), F32), V((4, nm // 2, nd, LANES), F32), V((3, nm // 2, nd, LANES), F32), V((nm // 2, nd, LANES), F32),
                 V((4, 8, 2, 8, 512), F32), V((2, 256, LANES), F32), V((256, LANES), F32), V((256, LANES), F32), V((2, 4, 32, LANES), F32),
                 V((8 * 32, LANES), F32), V((15, nd, LANES), F32),
-                dma((NT8,)), dma((3,)), dma, dma((npair,)), dma, dma, dma, dma, dma, dma, dma((3,)), dma((3,)), dma, dma, dma, dma],
+                dma((NT8,)), dma((3,)), dma, dma, dma((npair,)), dma, dma, dma, dma, dma, dma, dma((3,)), dma((3,)), dma, dma, dma, dma],
             compiler_params=pltpu.CompilerParams(collective_id=0, has_side_effects=True, vmem_limit_bytes=60 * 2**20),
         )(bt, mt, ct)
         return jnp.transpose(g, (1, 0, 2))

time: 75.6 us -> 71.8 us (0.950)
  Pallas kernels: 73.8 us -> 71 us
  local copies, waits for them, and re-layouts: 1.65 us -> 0.69 us
    pallas_call x1, Pallas kernels: 73.8 us -> 71 us  [local_fock(): pl.pallas_call(lambda *refs: kernel(nm, nl, nq, nd, ni, *refs), out_shape...]
    unnamed x1, local copies, waits for them, and re-layouts: 1.65 us -> 0.69 us
where the time goes in v17:
time: 71.8 us; the launch traced here: 71.7 us
  Pallas kernels  71 us (99%)
    pallas_call x1, Pallas kernels, local_fock(): pl.pallas_call(lambda *refs: kernel(nm, nl, nq, nd, ni, *refs), out_shape...  71 us

profile of v17, /device:TPU:0, one launch (start us, length us, event | category | flops | bytes accessed | tf_op | source)
XLA Modules:
  0.0 71.7 jit_solution(5493726804476735402)
XLA Ops:
  0.0 71.0 %shard_map.37 = f32[58,8,58]{2,1,0:T(8,128)S(1)} custom-call(f32[58,232,116]{2,1,0:T(8,128)} %bitcast.7, f32[464,116]{1,0:T(8,128)} %bitcast.8, f32[160,232]{1,0:T(8,128)} %bitcast.9), custom_call_target="tpu_custom_call" | custom-call | tf_op jit(solution)/shard_map/pallas_call | solution.py:404
  71.0 0.7 copy.5

commit v18 on v16

--- a/solution.py
+++ b/solution.py
@@ -165,7 +165,7 @@
     outer = jnp.logical_or(a == 0, a == 3)
     pair = a + 1 - 2 * (a % 2)
 
-    def send_half(p, t0, nt, cross):
+    def send_part(p, t0, nt, cross):
         def one(k, c):
             if cross:
                 aa = jnp.where(k % 2 == 0, 3 - a, 3 - pair)
@@ -191,6 +191,14 @@
             return c
         lax.fori_loop(0, 8, one, 0)
 
+    def send_half(p, t0, nt, cross):
+        send_part(p, t0, 4, cross)
+        send_part(p, t0 + 4, nt - 4, cross)
+
+    def send_both(p):
+        send_t1(p, 0, 4)
+        send_t1(p, 4, NT8 - 4)
+
     pltpu.make_async_copy(bt.at[pl.ds(0, 2)], bv.at[pl.ds(0, 2)], lsem.at[2]).wait()
 
     def two_tiles(u, gam):
@@ -238,7 +246,7 @@
     @pl.when(jnp.logical_not(outer))
     def _():
         for p in range(1, 3):
-            send_t1(p, 0, NT8)
+            send_both(p)
     mq[a] = mloc[...]
     for k in range(1, 4):
         c1 = lax.rem(a + k, 4)

time: 70.6 us -> 71.3 us (level)
  Pallas kernels: 69.7 us -> 70.5 us
    pallas_call x1, Pallas kernels: 69.7 us -> 70.5 us  [local_fock(): pl.pallas_call(lambda *refs: kernel(nm, nl, nq, nd, ni, *refs), out_shape...]
where the time goes in v18:
time: 71.3 us; the launch traced here: 71.2 us
  Pallas kernels  70.5 us (99%)
    pallas_call x1, Pallas kernels, local_fock(): pl.pallas_call(lambda *refs: kernel(nm, nl, nq, nd, ni, *refs), out_shape...  70.5 us

profile of v18, /device:TPU:0, one launch (start us, length us, event | category | flops | bytes accessed | tf_op | source)
XLA Modules:
  0.0 71.2 jit_solution(10323255280384442509)
XLA Ops:
  0.0 70.5 %shard_map.37 = f32[58,8,58]{2,1,0:T(8,128)S(1)} custom-call(f32[58,232,116]{2,1,0:T(8,128)} %bitcast.7, f32[464,116]{1,0:T(8,128)} %bitcast.8, f32[160,232]{1,0:T(8,128)} %bitcast.9), custom_call_target="tpu_custom_call" | custom-call | tf_op jit(solution)/shard_map/pallas_call | solution.py:440
  70.5 0.7 copy.5

commit v19 on v16

--- a/solution.py
+++ b/solution.py
@@ -195,17 +195,15 @@
 
     def two_tiles(u, gam):
         gam = tile(2 * u, gam, u, 0)
-        send_t1(0, 2 * u, 1)
         gam = tile(2 * u + 1, gam, u, 8)
-        send_t1(0, 2 * u + 1, 1)
+        send_t1(0, 2 * u, 2)
         return gam
     gam = lax.fori_loop(0, 2, two_tiles, gam)
 
     def one_tile(t, gam):
-        gam = tile(t, gam, None, 0)
-        send_t1(0, t, 1)
-        return gam
+        return tile(t, gam, None, 0)
     gam = lax.fori_loop(4, NT8, one_tile, gam)
+    send_t1(0, 4, NT8 - 4)
 
     gsend[...] = gam
 

time: 70.6 us -> 71.2 us (level)
  no operation moved by 1% of the time
where the time goes in v19:
time: 71.2 us; the launch traced here: 71.1 us
  Pallas kernels  70.3 us (99%)
    pallas_call x1, Pallas kernels, local_fock(): pl.pallas_call(lambda *refs: kernel(nm, nl, nq, nd, ni, *refs), out_shape...  70.3 us

profile of v19, /device:TPU:0, one launch (start us, length us, event | category | flops | bytes accessed | tf_op | source)
XLA Modules:
  0.0 71.1 jit_solution(14915408934731354433)
XLA Ops:
  0.0 70.3 %shard_map.37 = f32[58,8,58]{2,1,0:T(8,128)S(1)} custom-call(f32[58,232,116]{2,1,0:T(8,128)} %bitcast.7, f32[464,116]{1,0:T(8,128)} %bitcast.8, f32[160,232]{1,0:T(8,128)} %bitcast.9), custom_call_target="tpu_custom_call" | custom-call | tf_op jit(solution)/shard_map/pallas_call | solution.py:430
  70.4 0.7 copy.5

commit v20 on v16

--- a/solution.py
+++ b/solution.py
@@ -353,13 +353,21 @@
     def _():
         for p in range(3, npair):
             send_half(p, 0, NT8, False)
-    for p in range(npair - 1):
+    cross = pltpu.make_async_remote_copy(src_ref=jfwd, dst_ref=jrecv.at[2], send_sem=jssem.at[2], recv_sem=jrsem.at[2],
+                                         device_id=dev(far, o), device_id_type=MESH)
+    for p in range(3):
         fit(p)
     hops[0].wait_recv()
     jfwd[...] = jsend[far] + jrecv[0]
-    cross = pltpu.make_async_remote_copy(src_ref=jfwd, dst_ref=jrecv.at[2], send_sem=jssem.at[2], recv_sem=jrsem.at[2],
-                                         device_id=dev(far, o), device_id_type=MESH)
-    cross.start()
+
+    @pl.when(jnp.logical_not(outer))
+    def _():
+        cross.start()
+    fit(3)
+
+    @pl.when(outer)
+    def _():
+        cross.start()
     fit(npair - 1)
 
     mate = o + 1 - 2 * half

time: 70.6 us -> 70.6 us (level)
  no operation moved by 1% of the time
where the time goes in v20:
time: 70.6 us; the launch traced here: 70.5 us
  Pallas kernels  69.7 us (99%)
    pallas_call x1, Pallas kernels, local_fock(): pl.pallas_call(lambda *refs: kernel(nm, nl, nq, nd, ni, *refs), out_shape...  69.7 us

profile of v20, /device:TPU:0, one launch (start us, length us, event | category | flops | bytes accessed | tf_op | source)
XLA Modules:
  0.0 70.5 jit_solution(14362384556575919630)
XLA Ops:
  0.0 69.7 %shard_map.37 = f32[58,8,58]{2,1,0:T(8,128)S(1)} custom-call(f32[58,232,116]{2,1,0:T(8,128)} %bitcast.7, f32[464,116]{1,0:T(8,128)} %bitcast.8, f32[160,232]{1,0:T(8,128)} %bitcast.9), custom_call_target="tpu_custom_call" | custom-call | tf_op jit(solution)/shard_map/pallas_call | solution.py:440
  69.8 0.7 copy.5

commit v21 on v16

--- a/solution.py
+++ b/solution.py
@@ -38,7 +38,7 @@
     return jnp.concatenate([h, m, h, m, l, h], axis=axis)
 
 
-def kernel(nm, nl, nq, nd, ni, bt, mt, ct, out, bv, mv, cv, ctp, tr, sbuf, rbuf, own, mloc, mqr, mq, msp, gsend, grecv, jsend, jrecv, jfwd, zbuf, kacc, kin, kful, kmsg, krecv, gbuf,
+def kernel(nm, nl, nq, nd, ni, bt, mt, ct, out, bv, mv, cv, ctp, tr, sbuf, rbuf, own, mloc, mqr, mq, msp, gsend, grecv, jsend, jrecv, jfwd, zbuf, kacc, kin, kful, kmsg, krecv, gbuf, zown, sacc,
            bsem, lsem, tsend, trecv, mzsend, mzrecv, mosend, morecv, gssem, grsem, jssem, jrsem, kxs, kxr, kss, krs):
     sy, a, o = lax.axis_index('sys'), lax.axis_index('aux'), lax.axis_index('orb')
     me = a * 4 + o
@@ -301,6 +301,19 @@
         return out
 
     def fit(p):
+        ml = []
+        for s in range(2):
+            rest = tails(own[s, p, pl.ds(0, 4)]) + [jnp.zeros((12, LANES), F32)]
+            ml.append(jnp.concatenate([own[s, p].reshape(NT8 * 16, LANES), jnp.concatenate(rest, axis=0).astype(BF)], axis=0))
+        mid, low = ml
+        rows = pl.ds(pl.multiple_of(a * LANES, LANES), LANES)
+        mh, mm = msp[0, rows], msp[1, rows]
+        zown[...] = dot(jnp.concatenate([mid, mid, low], axis=1), jnp.concatenate([mh, mm, mh], axis=0), NN)
+        if p == npair - 1:
+            s = sacc[...]
+            s = s + s.T
+            kacc[0] = kacc[0] + s[:, :LANES]
+            kacc[1] = kacc[1] + s[:, LANES:]
         pltpu.make_async_copy(rbuf.at[:, p], rbuf.at[:, p], trecv.at[p]).wait()
         if p + 3 < npair:
             @pl.when(jnp.logical_not(outer))
@@ -317,20 +330,23 @@
         for q in range(4):
             for e in range(2):
                 zbuf[q, NT8, e, pl.ds(0, 2)] = z[main + 4 * q + 2 * e:main + 4 * q + 2 * e + 2]
-        ml = []
-        for s in range(2):
-            rest = tails(own[s, p, pl.ds(0, 4)]) + [jnp.zeros((12, LANES), F32)]
-            ml.append(jnp.concatenate([own[s, p].reshape(NT8 * 16, LANES), jnp.concatenate(rest, axis=0).astype(BF)], axis=0))
-        mid, low = ml
-        rows = pl.ds(pl.multiple_of(a * LANES, LANES), LANES)
-        mh, mm = msp[0, rows], msp[1, rows]
-        z = dot(jnp.concatenate([mid, mid, low], axis=1), jnp.concatenate([mh, mm, mh], axis=0), NN)
+        z = zown[...]
         zbuf[o, pl.ds(0, NT8)] = zbuf[o, pl.ds(0, NT8)] + z[:NT8 * 16].reshape(NT8, 2, 8, 512)
         for e in range(2):
             zbuf[o, NT8, e, pl.ds(0, 2)] = zbuf[o, NT8, e, pl.ds(0, 2)] + z[NT8 * 16 + 2 * e:NT8 * 16 + 2 * e + 2]
         for e in range(2):
             s3 = split3(zbuf[:, :, e].reshape(4 * MROW, 512))
-            k = dot(lhs6(s3, 1), rhs6(s3, 1), NT)
+            if p == npair - 1:
+                k = dot(lhs6(s3, 1), rhs6(s3, 1), NT)
+            else:
+                hi, mid, low = s3
+                both = jnp.concatenate([hi, mid], axis=1)
+                k = dot(both, both, NT)
+                half_sum = dot(jnp.concatenate([hi, hi], axis=1), jnp.concatenate([mid, low], axis=1), NT)
+                if p == 0 and e == 0:
+                    sacc[...] = half_sum
+                else:
+                    sacc[...] = sacc[...] + half_sum
             if p == 0 and e == 0:
                 kacc[0] = k[:, :LANES]
                 kacc[1] = k[:, LANES:]
@@ -369,28 +385,24 @@
     swap.wait_recv()
     kful[...] = kacc[half] + kin[...]
     low32 = lax.broadcasted_iota(jnp.int32, (32, LANES), 1) < 64
+    kland = krecv.at[pl.ds(pl.multiple_of(dens * 32, 32), 32)]
     for oo in range(4):
         ev = kful[pl.ds(MROW * oo, 32, stride=2), :]
         od = kful[pl.ds(MROW * oo + 1, 32, stride=2), :]
         kmsg[0, oo] = jnp.where(low32, ev, pltpu.roll(od, 64, 1))
         kmsg[1, oo] = jnp.where(low32, pltpu.roll(ev, 64, 1), od)
-
-    def ks(k, c):
-        al, oo = k // 4, k % 4
-        aa = 2 * half + al
-        same = jnp.logical_and(aa == a, oo == o)
-
-        @pl.when(jnp.logical_not(same))
-        def _():
-            pltpu.make_async_remote_copy(src_ref=kmsg.at[al, oo], dst_ref=krecv.at[pl.ds(dens * 32, 32)], send_sem=kss, recv_sem=krs,
-                                         device_id=dev(aa, oo), device_id_type=MESH).start()
-
-        @pl.when(same)
-        def _():
-            cp = pltpu.make_async_copy(kmsg.at[al, oo], krecv.at[pl.ds(dens * 32, 32)], krs)
-            cp.start()
-        return c
-    lax.fori_loop(0, 8, ks, 0)
+        for al in range(2):
+            aa = 2 * half + al
+            same = jnp.logical_and(aa == a, oo == o)
+
+            @pl.when(jnp.logical_not(same))
+            def _():
+                pltpu.make_async_remote_copy(src_ref=kmsg.at[al, oo], dst_ref=kland, send_sem=kss, recv_sem=krs,
+                                             device_id=dev(aa, oo), device_id_type=MESH).start()
+
+            @pl.when(same)
+            def _():
+                pltpu.make_async_copy(kmsg.at[al, oo], kland, krs).start()
 
     hops[1].wait_recv()
     cross.wait_recv()
@@ -440,7 +452,7 @@
                 V((2, npair, NT8, 16, LANES), BF), V((4, LANES, LANES), F32), V((6, LANES, LANES), F32), V((4, 4, LANES, LANES), F32), V((3, 512, 512), BF),
                 V((nd, LANES), F32), V((4, 4, nd, LANES), F32), V((4, nm // 2, nd, LANES), F32), V((3, nm // 2, nd, LANES), F32), V((nm // 2, nd, LANES), F32),
                 V((4, 8, 2, 8, 512), F32), V((2, 256, LANES), F32), V((256, LANES), F32), V((256, LANES), F32), V((2, 4, 32, LANES), F32),
-                V((8 * 32, LANES), F32), V((15, nd, LANES), F32),
+                V((8 * 32, LANES), F32), V((15, nd, LANES), F32), V((LANES, 512), F32), V((256, 256), F32),
                 dma((NT8,)), dma((3,)), dma, dma((npair,)), dma, dma, dma, dma, dma, dma, dma((3,)), dma((3,)), dma, dma, dma, dma],
             compiler_params=pltpu.CompilerParams(collective_id=0, has_side_effects=True, vmem_limit_bytes=60 * 2**20),
         )(bt, mt, ct)

time: 70.6 us -> 72 us (1.020)
  Pallas kernels: 69.7 us -> 71.2 us
    pallas_call x1, Pallas kernels: 69.7 us -> 71.2 us  [local_fock(): pl.pallas_call(lambda *refs: kernel(nm, nl, nq, nd, ni, *refs), out_shape...]
where the time goes in v21:
time: 72 us; the launch traced here: 71.9 us
  Pallas kernels  71.2 us (99%)
    pallas_call x1, Pallas kernels, local_fock(): pl.pallas_call(lambda *refs: kernel(nm, nl, nq, nd, ni, *refs), out_shape...  71.2 us

profile of v21, /device:TPU:0, one launch (start us, length us, event | category | flops | bytes accessed | tf_op | source)
XLA Modules:
  0.0 71.9 jit_solution(5441576291104346609)
XLA Ops:
  0.0 71.2 %shard_map.37 = f32[58,8,58]{2,1,0:T(8,128)S(1)} custom-call(f32[58,232,116]{2,1,0:T(8,128)} %bitcast.7, f32[464,116]{1,0:T(8,128)} %bitcast.8, f32[160,232]{1,0:T(8,128)} %bitcast.9), custom_call_target="tpu_custom_call" | custom-call | tf_op jit(solution)/shard_map/pallas_call | solution.py:444
  71.2 0.7 copy.5

commit v22 on v21

--- a/solution.py
+++ b/solution.py
@@ -315,10 +315,10 @@
             kacc[0] = kacc[0] + s[:, :LANES]
             kacc[1] = kacc[1] + s[:, LANES:]
         pltpu.make_async_copy(rbuf.at[:, p], rbuf.at[:, p], trecv.at[p]).wait()
-        if p + 3 < npair:
+        if p in (0, 2):
             @pl.when(jnp.logical_not(outer))
             def _():
-                send_half(p + 3, 0, NT8, True)
+                send_half(3 if p == 0 else 4, 0, NT8, True)
         xs = []
         for s in range(4):
             rest = [w for q in range(4) for w in tails(rbuf[s, p, q, pl.ds(0, 4)])]
@@ -385,24 +385,28 @@
     swap.wait_recv()
     kful[...] = kacc[half] + kin[...]
     low32 = lax.broadcasted_iota(jnp.int32, (32, LANES), 1) < 64
-    kland = krecv.at[pl.ds(pl.multiple_of(dens * 32, 32), 32)]
     for oo in range(4):
         ev = kful[pl.ds(MROW * oo, 32, stride=2), :]
         od = kful[pl.ds(MROW * oo + 1, 32, stride=2), :]
         kmsg[0, oo] = jnp.where(low32, ev, pltpu.roll(od, 64, 1))
         kmsg[1, oo] = jnp.where(low32, pltpu.roll(ev, 64, 1), od)
-        for al in range(2):
-            aa = 2 * half + al
-            same = jnp.logical_and(aa == a, oo == o)
-
-            @pl.when(jnp.logical_not(same))
-            def _():
-                pltpu.make_async_remote_copy(src_ref=kmsg.at[al, oo], dst_ref=kland, send_sem=kss, recv_sem=krs,
-                                             device_id=dev(aa, oo), device_id_type=MESH).start()
-
-            @pl.when(same)
-            def _():
-                pltpu.make_async_copy(kmsg.at[al, oo], kland, krs).start()
+
+    def ks(k, c):
+        al, oo = k // 4, k % 4
+        aa = 2 * half + al
+        same = jnp.logical_and(aa == a, oo == o)
+
+        @pl.when(jnp.logical_not(same))
+        def _():
+            pltpu.make_async_remote_copy(src_ref=kmsg.at[al, oo], dst_ref=krecv.at[pl.ds(dens * 32, 32)], send_sem=kss, recv_sem=krs,
+                                         device_id=dev(aa, oo), device_id_type=MESH).start()
+
+        @pl.when(same)
+        def _():
+            cp = pltpu.make_async_copy(kmsg.at[al, oo], krecv.at[pl.ds(dens * 32, 32)], krs)
+            cp.start()
+        return c
+    lax.fori_loop(0, 8, ks, 0)
 
     hops[1].wait_recv()
     cross.wait_recv()

time: 72 us -> 72 us (level)
  no operation moved by 1% of the time
where the time goes in v22:
time: 72 us; the launch traced here: 71.9 us
  Pallas kernels  71.2 us (99%)
    pallas_call x1, Pallas kernels, local_fock(): pl.pallas_call(lambda *refs: kernel(nm, nl, nq, nd, ni, *refs), out_shape...  71.2 us

profile of v22, /device:TPU:0, one launch (start us, length us, event | category | flops | bytes accessed | tf_op | source)
XLA Modules:
  0.0 71.9 jit_solution(12823303077809774705)
XLA Ops:
  0.0 71.2 %shard_map.37 = f32[58,8,58]{2,1,0:T(8,128)S(1)} custom-call(f32[58,232,116]{2,1,0:T(8,128)} %bitcast.7, f32[464,116]{1,0:T(8,128)} %bitcast.8, f32[160,232]{1,0:T(8,128)} %bitcast.9), custom_call_target="tpu_custom_call" | custom-call | tf_op jit(solution)/shard_map/pallas_call | solution.py:448
  71.2 0.7 copy.5

commit v23 on v16

--- a/solution.py
+++ b/solution.py
@@ -66,36 +66,6 @@
     pltpu.make_async_copy(ct, cv, lsem.at[0]).wait()
     ctp[...] = jnp.concatenate([cv[...], jnp.zeros((nd * ni, 256 - nl), F32)], axis=1)
     lhs = lhs6(split3(ctp[...]), 1)
-    pltpu.make_async_copy(mt, mv, lsem.at[1]).wait()
-    for b in range(4):
-        blk = jnp.concatenate([mv[nq * b:nq * (b + 1), :], jnp.zeros((nq, LANES - nq), F32)], axis=1)
-        mloc[b] = jnp.concatenate([blk, jnp.zeros((LANES - nq, LANES), F32)], axis=0)
-    pl.semaphore_wait(barrier, 15)
-
-    quarter = pl.ds(pl.multiple_of(o * 32, 32), 32)
-
-    def nearer(x, y, z):
-        dx, dy = jnp.abs(x - z), jnp.abs(y - z)
-        return jnp.logical_or(dx < dy, jnp.logical_and(dx == dy, x < y))
-
-    def metric_copies(act):
-        for k in (2, 1, 3):
-            to = lax.rem(a + 4 - k, 4)
-
-            def block(row, slot):
-                return pltpu.make_async_remote_copy(src_ref=mloc.at[row, quarter], dst_ref=mqr.at[slot, quarter], send_sem=mzsend,
-                                                    recv_sem=mzrecv, device_id=dev(to, o), device_id_type=MESH)
-            act(block(a, k - 1))
-            for k2 in (1, 2, 3):
-                if k2 == k:
-                    continue
-                b = lax.rem(to + k2, 4)
-
-                @pl.when(nearer(a, b, to))
-                def _():
-                    act(block(b, k + k2))
-    metric_copies(lambda c: c.start())
-
     gam = jnp.zeros((nd, LANES), F32)
     tr2 = tr
 
@@ -193,13 +163,44 @@
 
     pltpu.make_async_copy(bt.at[pl.ds(0, 2)], bv.at[pl.ds(0, 2)], lsem.at[2]).wait()
 
-    def two_tiles(u, gam):
-        gam = tile(2 * u, gam, u, 0)
-        send_t1(0, 2 * u, 1)
-        gam = tile(2 * u + 1, gam, u, 8)
-        send_t1(0, 2 * u + 1, 1)
-        return gam
-    gam = lax.fori_loop(0, 2, two_tiles, gam)
+    gam = tile(0, gam, 0, 0)
+    pltpu.make_async_copy(mt, mv, lsem.at[1]).wait()
+    for b in range(4):
+        blk = jnp.concatenate([mv[nq * b:nq * (b + 1), :], jnp.zeros((nq, LANES - nq), F32)], axis=1)
+        mloc[b] = jnp.concatenate([blk, jnp.zeros((LANES - nq, LANES), F32)], axis=0)
+    pl.semaphore_wait(barrier, 15)
+
+    quarter = pl.ds(pl.multiple_of(o * 32, 32), 32)
+
+    def nearer(x, y, z):
+        dx, dy = jnp.abs(x - z), jnp.abs(y - z)
+        return jnp.logical_or(dx < dy, jnp.logical_and(dx == dy, x < y))
+
+    def metric_copies(act):
+        for k in (2, 1, 3):
+            to = lax.rem(a + 4 - k, 4)
+
+            def block(row, slot):
+                return pltpu.make_async_remote_copy(src_ref=mloc.at[row, quarter], dst_ref=mqr.at[slot, quarter], send_sem=mzsend,
+                                                    recv_sem=mzrecv, device_id=dev(to, o), device_id_type=MESH)
+            act(block(a, k - 1))
+            for k2 in (1, 2, 3):
+                if k2 == k:
+                    continue
+                b = lax.rem(to + k2, 4)
+
+                @pl.when(nearer(a, b, to))
+                def _():
+                    act(block(b, k + k2))
+    metric_copies(lambda c: c.start())
+
+    send_t1(0, 0, 1)
+    gam = tile(1, gam, 0, 8)
+    send_t1(0, 1, 1)
+    gam = tile(2, gam, 1, 0)
+    send_t1(0, 2, 1)
+    gam = tile(3, gam, 1, 8)
+    send_t1(0, 3, 1)
 
     def one_tile(t, gam):
         gam = tile(t, gam, None, 0)

time: 70.6 us -> 71.9 us (1.018)
  Pallas kernels: 69.7 us -> 71.1 us
    pallas_call x1, Pallas kernels: 69.7 us -> 71.1 us  [local_fock(): pl.pallas_call(lambda *refs: kernel(nm, nl, nq, nd, ni, *refs), out_shape...]
where the time goes in v23:
time: 71.9 us; the launch traced here: 71.8 us
  Pallas kernels  71.1 us (99%)
    pallas_call x1, Pallas kernels, local_fock(): pl.pallas_call(lambda *refs: kernel(nm, nl, nq, nd, ni, *refs), out_shape...  71.1 us

profile of v23, /device:TPU:0, one launch (start us, length us, event | category | flops | bytes accessed | tf_op | source)
XLA Modules:
  0.0 71.8 jit_solution(529767096607268184)
XLA Ops:
  0.0 71.1 %shard_map.37 = f32[58,8,58]{2,1,0:T(8,128)S(1)} custom-call(f32[58,232,116]{2,1,0:T(8,128)} %bitcast.7, f32[464,116]{1,0:T(8,128)} %bitcast.8, f32[160,232]{1,0:T(8,128)} %bitcast.9), custom_call_target="tpu_custom_call" | custom-call | tf_op jit(solution)/shard_map/pallas_call | solution.py:433
  71.1 0.7 copy.5

commit v24 on v16

--- a/solution.py
+++ b/solution.py
@@ -49,12 +49,11 @@
     def dev(aa, oo):
         return (sy, aa, oo)
 
+    pltpu.make_async_copy(mt, mv, lsem.at[1]).start()
     pltpu.make_async_copy(ct, cv, lsem.at[0]).start()
     pltpu.make_async_copy(bt.at[pl.ds(8 * NT8, 2)], bv.at[pl.ds(8 * NT8, 2)], lsem.at[2]).start()
     for t in range(NT8):
         pltpu.make_async_copy(bt.at[pl.ds(8 * t, 8)], bv.at[pl.ds(8 * t, 8)], bsem.at[t]).start()
-        if t == 0:
-            pltpu.make_async_copy(mt, mv, lsem.at[1]).start()
     barrier = pltpu.get_barrier_semaphore()
 
     def tell(k, c):
@@ -63,9 +62,6 @@
         return c
     lax.fori_loop(1, 16, tell, 0)
 
-    pltpu.make_async_copy(ct, cv, lsem.at[0]).wait()
-    ctp[...] = jnp.concatenate([cv[...], jnp.zeros((nd * ni, 256 - nl), F32)], axis=1)
-    lhs = lhs6(split3(ctp[...]), 1)
     pltpu.make_async_copy(mt, mv, lsem.at[1]).wait()
     for b in range(4):
         blk = jnp.concatenate([mv[nq * b:nq * (b + 1), :], jnp.zeros((nq, LANES - nq), F32)], axis=1)
@@ -95,6 +91,10 @@
                 def _():
                     act(block(b, k + k2))
     metric_copies(lambda c: c.start())
+
+    pltpu.make_async_copy(ct, cv, lsem.at[0]).wait()
+    ctp[...] = jnp.concatenate([cv[...], jnp.zeros((nd * ni, 256 - nl), F32)], axis=1)
+    lhs = lhs6(split3(ctp[...]), 1)
 
     gam = jnp.zeros((nd, LANES), F32)
     tr2 = tr

time: 70.6 us -> 70.9 us (level)
  no operation moved by 1% of the time
where the time goes in v24:
time: 70.9 us; the launch traced here: 70.8 us
  Pallas kernels  70.1 us (99%)
    pallas_call x1, Pallas kernels, local_fock(): pl.pallas_call(lambda *refs: kernel(nm, nl, nq, nd, ni, *refs), out_shape...  70.1 us

profile of v24, /device:TPU:0, one launch (start us, length us, event | category | flops | bytes accessed | tf_op | source)
XLA Modules:
  0.0 70.8 jit_solution(792495494975621254)
XLA Ops:
  0.0 70.1 %shard_map.37 = f32[58,8,58]{2,1,0:T(8,128)S(1)} custom-call(f32[58,232,116]{2,1,0:T(8,128)} %bitcast.7, f32[464,116]{1,0:T(8,128)} %bitcast.8, f32[160,232]{1,0:T(8,128)} %bitcast.9), custom_call_target="tpu_custom_call" | custom-call | tf_op jit(solution)/shard_map/pallas_call | solution.py:432
  70.1 0.7 copy.5
